TPU v7x, 256 devices: a 8x8x2 block of a 8x8x16 slice. The times are simulated.
256 devices in a mesh: grp: 2 (over z), blk: 128 (over y, x, core).
Axes of the slice: x: 8, y: 8, z: 2, core: 2. Of those that a mesh axis runs over, the one named last changes fastest.
The devices are a block of a 8x8x16 slice.
Arguments:
- example_grads: bfloat16 [256, 1048576], P('grp', 'blk'), parts along dimension 0, may hold values from -6 to 6
- tile_seeds: int32 [2048, 8], P('blk'), may hold values from 0 to 16777215
- pair_index: int32 [128, 2], P('grp'), parts along dimension 0, may hold values from 0 to 127
Outputs:
- projected: float32 [4096, 256], P('blk', 'grp'), parts along dimension 1
- scores: float32 [128], P('grp'), parts along dimension 0
There are 2 independent parts, one for each index of `grp`. A program takes and returns all parts, laid end to end along the dimension named above; an argument that names none is the same for every part. Nothing has to cross between parts.
Inputs may be any that keep to these rules, and one draw needn't show every extreme that they name: `pair_index`: column 0 names the query example and column 1 the negative example.
All inputs are finite; a program needn't handle non-finite values.
Results may differ from a plain program's by a relative error of at most 0.0003.
Values sent between devices are 32-bit elements; how exact they have to be, the bound alone decides.
No kernel may reach another device: no remote copies, remote signals or barrier semaphores. Data moves between devices by JAX's collectives and lax.ppermute only.
A program may use at most 64 MiB of HBM per device.

v0:
```python
import math

import jax
import jax.numpy as jnp
from jax import lax
from jax.sharding import PartitionSpec as P

TILE = 512


golden_mult = -1640531535
mixer_one = -2048144789
mixer_two = -1028477387


def hashed(seed_value, flat_index):
    mixed = seed_value ^ flat_index * jnp.int32(golden_mult)
    mixed = mixed ^ lax.shift_right_logical(mixed, jnp.int32(16))
    mixed = mixed * jnp.int32(mixer_one)
    mixed = mixed ^ lax.shift_right_logical(mixed, jnp.int32(13))
    mixed = mixed * jnp.int32(mixer_two)
    mixed = mixed ^ lax.shift_right_logical(mixed, jnp.int32(16))
    bit_value = lax.shift_right_logical(mixed, jnp.int32(15)) & jnp.int32(1)
    return jnp.int32(1) - jnp.int32(2) * bit_value


def pair_products(columns, pair_index, examples):
    example_ids = jnp.arange(examples, dtype=jnp.int32)
    pick_query = (pair_index[:, 0][:, None] == example_ids[None, :]).astype(jnp.float32)
    pick_negative = (pair_index[:, 1][:, None] == example_ids[None, :]).astype(jnp.float32)
    query_cols = jnp.dot(columns, pick_query.T, precision=lax.Precision.HIGHEST)
    negative_cols = jnp.dot(columns, pick_negative.T, precision=lax.Precision.HIGHEST)
    return jnp.sum(query_cols * negative_cols, axis=0)


def per_device(example_grads, tile_seeds, pair_index):
    examples, params = example_grads.shape
    devices = lax.axis_size("blk")
    col_total = tile_seeds.shape[1] * TILE
    scaling = 1.0 / math.sqrt(params * devices)
    row_ids = jnp.arange(TILE, dtype=jnp.int32)
    own_count = col_total // devices
    col_ids = jnp.arange(col_total, dtype=jnp.int32)
    flat_index = row_ids[:, None] * TILE + (col_ids % TILE)[None, :]

    def advance(tile_pos, running):
        seed_row = lax.dynamic_index_in_dim(tile_seeds, tile_pos, 0, keepdims=False)
        seed_full = jnp.broadcast_to(seed_row[:, None], (col_total // TILE, TILE)).reshape(
            col_total
        )
        sign_tile = hashed(seed_full[None, :], flat_index).astype(jnp.bfloat16)
        grad_block = lax.dynamic_slice_in_dim(example_grads, tile_pos * TILE, TILE, 1)
        return running + lax.dot_general(
            sign_tile, grad_block, (((0,), (1,)), ((), ())), preferred_element_type=jnp.float32
        )

    running = lax.fori_loop(
        0, params // TILE, advance, jnp.zeros((col_total, examples), jnp.float32)
    )
    everything = lax.psum(running * scaling, "blk")
    scores = pair_products(everything, pair_index, examples) * (1.0 / math.sqrt(col_total))
    own_rows = lax.dynamic_slice_in_dim(everything, lax.axis_index("blk") * own_count, own_count, 0)
    return (own_rows, scores)


def solution(mesh):
    placed = (P("grp", "blk"), P("blk", None), P("grp", None))
    return jax.shard_map(
        per_device,
        mesh=mesh,
        in_specs=placed,
        out_specs=(P("blk", "grp"), P("grp")),
        check_vma=False,
    )
```

profile of v0, /device:TPU:513, one launch (start us, length us, event | category | flops | bytes accessed | tf_op | source)
XLA Modules:
  0.0 332.6 jit_solution(8385331971153140161)
XLA Ops:
  7.2 0.1 all-reduce.2.cloned.1.call-start
  7.3 0.8 copy.5
  8.0 96.3 %while.14 = (s32[]{:T(128)}, f32[4096,128]{1,0:T(8,128)S(1)}, s32[16,8]{1,0:T(8,128)S(1)}, bf16[128,8192]{1,0:T(8,128)(2,1)}, s32[4096]{0:T(1024)S(1)}, /*index=...) while((s32[]{:T(128)}, f32[4096,128]{1,0:T(8,128)S(1)}, s32[16,8]{1,0:T(8,128)S(1)}, ...), condition=%wide.region_1.2_spmd.clone, body=%wide.region_0.1_spmd.clone.sunk | while | flops 571473920 | bytes 4409613 | solution.py:57
  8.0 0.1 broadcast_bitcast_fusion.2
  8.1 5.9 %convolution_add_fusion.2 = f32[4096,128]{1,0:T(8,128)S(1)} fusion(s32[4096]{0:T(1024)S(1)} %get-tuple-element.203, s32[512]{0:T(512)S(1)} %get-tuple-element.204, s32[4096]{0:T(1024)S(1)} %bitcast.17, f32[4096,128]{1,0:T(8,128)S(1)} %get-tuple-element.190, pred[]{:T(512)S(6)} %compare.4, bf16[128,8192]{1,0:T(8,128)(2,1)} %get-tuple-element.202, ...), kind=kOutput, calls=%fused_computation.13.clone.1 | convolution fusion | flops 571473920 | bytes 4360197 | tf_op jit(solution)/shard_map/while/body/eval_jaxpr/dot_general | solution.py:53
  14.1 0.1 broadcast_bitcast_fusion.2
  14.1 5.9 %convolution_add_fusion.2 = f32[4096,128]{1,0:T(8,128)S(1)} fusion(s32[4096]{0:T(1024)S(1)} %get-tuple-element.203, s32[512]{0:T(512)S(1)} %get-tuple-element.204, s32[4096]{0:T(1024)S(1)} %bitcast.17, f32[4096,128]{1,0:T(8,128)S(1)} %get-tuple-element.190, pred[]{:T(512)S(6)} %compare.4, bf16[128,8192]{1,0:T(8,128)(2,1)} %get-tuple-element.202, ...), kind=kOutput, calls=%fused_computation.13.clone.1 | convolution fusion | flops 571473920 | bytes 4360197 | tf_op jit(solution)/shard_map/while/body/eval_jaxpr/dot_general | solution.py:53
  20.1 0.1 broadcast_bitcast_fusion.2
  20.2 5.9 %convolution_add_fusion.2 = f32[4096,128]{1,0:T(8,128)S(1)} fusion(s32[4096]{0:T(1024)S(1)} %get-tuple-element.203, s32[512]{0:T(512)S(1)} %get-tuple-element.204, s32[4096]{0:T(1024)S(1)} %bitcast.17, f32[4096,128]{1,0:T(8,128)S(1)} %get-tuple-element.190, pred[]{:T(512)S(6)} %compare.4, bf16[128,8192]{1,0:T(8,128)(2,1)} %get-tuple-element.202, ...), kind=kOutput, calls=%fused_computation.13.clone.1 | convolution fusion | flops 571473920 | bytes 4360197 | tf_op jit(solution)/shard_map/while/body/eval_jaxpr/dot_general | solution.py:53
  26.1 0.1 broadcast_bitcast_fusion.2
  26.2 5.9 %convolution_add_fusion.2 = f32[4096,128]{1,0:T(8,128)S(1)} fusion(s32[4096]{0:T(1024)S(1)} %get-tuple-element.203, s32[512]{0:T(512)S(1)} %get-tuple-element.204, s32[4096]{0:T(1024)S(1)} %bitcast.17, f32[4096,128]{1,0:T(8,128)S(1)} %get-tuple-element.190, pred[]{:T(512)S(6)} %compare.4, bf16[128,8192]{1,0:T(8,128)(2,1)} %get-tuple-element.202, ...), kind=kOutput, calls=%fused_computation.13.clone.1 | convolution fusion | flops 571473920 | bytes 4360197 | tf_op jit(solution)/shard_map/while/body/eval_jaxpr/dot_general | solution.py:53
  32.1 0.1 broadcast_bitcast_fusion.2
  32.2 5.9 %convolution_add_fusion.2 = f32[4096,128]{1,0:T(8,128)S(1)} fusion(s32[4096]{0:T(1024)S(1)} %get-tuple-element.203, s32[512]{0:T(512)S(1)} %get-tuple-element.204, s32[4096]{0:T(1024)S(1)} %bitcast.17, f32[4096,128]{1,0:T(8,128)S(1)} %get-tuple-element.190, pred[]{:T(512)S(6)} %compare.4, bf16[128,8192]{1,0:T(8,128)(2,1)} %get-tuple-element.202, ...), kind=kOutput, calls=%fused_computation.13.clone.1 | convolution fusion | flops 571473920 | bytes 4360197 | tf_op jit(solution)/shard_map/while/body/eval_jaxpr/dot_general | solution.py:53
  38.1 0.1 broadcast_bitcast_fusion.2
  38.2 5.9 %convolution_add_fusion.2 = f32[4096,128]{1,0:T(8,128)S(1)} fusion(s32[4096]{0:T(1024)S(1)} %get-tuple-element.203, s32[512]{0:T(512)S(1)} %get-tuple-element.204, s32[4096]{0:T(1024)S(1)} %bitcast.17, f32[4096,128]{1,0:T(8,128)S(1)} %get-tuple-element.190, pred[]{:T(512)S(6)} %compare.4, bf16[128,8192]{1,0:T(8,128)(2,1)} %get-tuple-element.202, ...), kind=kOutput, calls=%fused_computation.13.clone.1 | convolution fusion | flops 571473920 | bytes 4360197 | tf_op jit(solution)/shard_map/while/body/eval_jaxpr/dot_general | solution.py:53
  44.2 0.1 broadcast_bitcast_fusion.2
  44.2 5.9 %convolution_add_fusion.2 = f32[4096,128]{1,0:T(8,128)S(1)} fusion(s32[4096]{0:T(1024)S(1)} %get-tuple-element.203, s32[512]{0:T(512)S(1)} %get-tuple-element.204, s32[4096]{0:T(1024)S(1)} %bitcast.17, f32[4096,128]{1,0:T(8,128)S(1)} %get-tuple-element.190, pred[]{:T(512)S(6)} %compare.4, bf16[128,8192]{1,0:T(8,128)(2,1)} %get-tuple-element.202, ...), kind=kOutput, calls=%fused_computation.13.clone.1 | convolution fusion | flops 571473920 | bytes 4360197 | tf_op jit(solution)/shard_map/while/body/eval_jaxpr/dot_general | solution.py:53
  50.2 0.1 broadcast_bitcast_fusion.2
  50.3 5.9 %convolution_add_fusion.2 = f32[4096,128]{1,0:T(8,128)S(1)} fusion(s32[4096]{0:T(1024)S(1)} %get-tuple-element.203, s32[512]{0:T(512)S(1)} %get-tuple-element.204, s32[4096]{0:T(1024)S(1)} %bitcast.17, f32[4096,128]{1,0:T(8,128)S(1)} %get-tuple-element.190, pred[]{:T(512)S(6)} %compare.4, bf16[128,8192]{1,0:T(8,128)(2,1)} %get-tuple-element.202, ...), kind=kOutput, calls=%fused_computation.13.clone.1 | convolution fusion | flops 571473920 | bytes 4360197 | tf_op jit(solution)/shard_map/while/body/eval_jaxpr/dot_general | solution.py:53
  56.2 0.1 broadcast_bitcast_fusion.2
  56.3 5.9 %convolution_add_fusion.2 = f32[4096,128]{1,0:T(8,128)S(1)} fusion(s32[4096]{0:T(1024)S(1)} %get-tuple-element.203, s32[512]{0:T(512)S(1)} %get-tuple-element.204, s32[4096]{0:T(1024)S(1)} %bitcast.17, f32[4096,128]{1,0:T(8,128)S(1)} %get-tuple-element.190, pred[]{:T(512)S(6)} %compare.4, bf16[128,8192]{1,0:T(8,128)(2,1)} %get-tuple-element.202, ...), kind=kOutput, calls=%fused_computation.13.clone.1 | convolution fusion | flops 571473920 | bytes 4360197 | tf_op jit(solution)/shard_map/while/body/eval_jaxpr/dot_general | solution.py:53
  62.2 0.1 broadcast_bitcast_fusion.2
  62.3 5.9 %convolution_add_fusion.2 = f32[4096,128]{1,0:T(8,128)S(1)} fusion(s32[4096]{0:T(1024)S(1)} %get-tuple-element.203, s32[512]{0:T(512)S(1)} %get-tuple-element.204, s32[4096]{0:T(1024)S(1)} %bitcast.17, f32[4096,128]{1,0:T(8,128)S(1)} %get-tuple-element.190, pred[]{:T(512)S(6)} %compare.4, bf16[128,8192]{1,0:T(8,128)(2,1)} %get-tuple-element.202, ...), kind=kOutput, calls=%fused_computation.13.clone.1 | convolution fusion | flops 571473920 | bytes 4360197 | tf_op jit(solution)/shard_map/while/body/eval_jaxpr/dot_general | solution.py:53
  68.3 0.1 broadcast_bitcast_fusion.2
  68.3 5.9 %convolution_add_fusion.2 = f32[4096,128]{1,0:T(8,128)S(1)} fusion(s32[4096]{0:T(1024)S(1)} %get-tuple-element.203, s32[512]{0:T(512)S(1)} %get-tuple-element.204, s32[4096]{0:T(1024)S(1)} %bitcast.17, f32[4096,128]{1,0:T(8,128)S(1)} %get-tuple-element.190, pred[]{:T(512)S(6)} %compare.4, bf16[128,8192]{1,0:T(8,128)(2,1)} %get-tuple-element.202, ...), kind=kOutput, calls=%fused_computation.13.clone.1 | convolution fusion | flops 571473920 | bytes 4360197 | tf_op jit(solution)/shard_map/while/body/eval_jaxpr/dot_general | solution.py:53
  74.3 0.1 broadcast_bitcast_fusion.2
  74.4 5.9 %convolution_add_fusion.2 = f32[4096,128]{1,0:T(8,128)S(1)} fusion(s32[4096]{0:T(1024)S(1)} %get-tuple-element.203, s32[512]{0:T(512)S(1)} %get-tuple-element.204, s32[4096]{0:T(1024)S(1)} %bitcast.17, f32[4096,128]{1,0:T(8,128)S(1)} %get-tuple-element.190, pred[]{:T(512)S(6)} %compare.4, bf16[128,8192]{1,0:T(8,128)(2,1)} %get-tuple-element.202, ...), kind=kOutput, calls=%fused_computation.13.clone.1 | convolution fusion | flops 571473920 | bytes 4360197 | tf_op jit(solution)/shard_map/while/body/eval_jaxpr/dot_general | solution.py:53
  80.3 0.1 broadcast_bitcast_fusion.2
  80.4 5.9 %convolution_add_fusion.2 = f32[4096,128]{1,0:T(8,128)S(1)} fusion(s32[4096]{0:T(1024)S(1)} %get-tuple-element.203, s32[512]{0:T(512)S(1)} %get-tuple-element.204, s32[4096]{0:T(1024)S(1)} %bitcast.17, f32[4096,128]{1,0:T(8,128)S(1)} %get-tuple-element.190, pred[]{:T(512)S(6)} %compare.4, bf16[128,8192]{1,0:T(8,128)(2,1)} %get-tuple-element.202, ...), kind=kOutput, calls=%fused_computation.13.clone.1 | convolution fusion | flops 571473920 | bytes 4360197 | tf_op jit(solution)/shard_map/while/body/eval_jaxpr/dot_general | solution.py:53
  86.3 0.1 broadcast_bitcast_fusion.2
  86.4 5.9 %convolution_add_fusion.2 = f32[4096,128]{1,0:T(8,128)S(1)} fusion(s32[4096]{0:T(1024)S(1)} %get-tuple-element.203, s32[512]{0:T(512)S(1)} %get-tuple-element.204, s32[4096]{0:T(1024)S(1)} %bitcast.17, f32[4096,128]{1,0:T(8,128)S(1)} %get-tuple-element.190, pred[]{:T(512)S(6)} %compare.4, bf16[128,8192]{1,0:T(8,128)(2,1)} %get-tuple-element.202, ...), kind=kOutput, calls=%fused_computation.13.clone.1 | convolution fusion | flops 571473920 | bytes 4360197 | tf_op jit(solution)/shard_map/while/body/eval_jaxpr/dot_general | solution.py:53
  92.3 0.1 broadcast_bitcast_fusion.2
  92.4 5.9 %convolution_add_fusion.2 = f32[4096,128]{1,0:T(8,128)S(1)} fusion(s32[4096]{0:T(1024)S(1)} %get-tuple-element.203, s32[512]{0:T(512)S(1)} %get-tuple-element.204, s32[4096]{0:T(1024)S(1)} %bitcast.17, f32[4096,128]{1,0:T(8,128)S(1)} %get-tuple-element.190, pred[]{:T(512)S(6)} %compare.4, bf16[128,8192]{1,0:T(8,128)(2,1)} %get-tuple-element.202, ...), kind=kOutput, calls=%fused_computation.13.clone.1 | convolution fusion | flops 571473920 | bytes 4360197 | tf_op jit(solution)/shard_map/while/body/eval_jaxpr/dot_general | solution.py:53
  98.4 0.1 broadcast_bitcast_fusion.2
  98.4 5.9 %convolution_add_fusion.2 = f32[4096,128]{1,0:T(8,128)S(1)} fusion(s32[4096]{0:T(1024)S(1)} %get-tuple-element.203, s32[512]{0:T(512)S(1)} %get-tuple-element.204, s32[4096]{0:T(1024)S(1)} %bitcast.17, f32[4096,128]{1,0:T(8,128)S(1)} %get-tuple-element.190, pred[]{:T(512)S(6)} %compare.4, bf16[128,8192]{1,0:T(8,128)(2,1)} %get-tuple-element.202, ...), kind=kOutput, calls=%fused_computation.13.clone.1 | convolution fusion | flops 571473920 | bytes 4360197 | tf_op jit(solution)/shard_map/while/body/eval_jaxpr/dot_general | solution.py:53
  104.4 1.4 broadcast_multiply_fusion
  105.8 0.0 copy-start.1
  105.8 0.1 all-reduce.2.cloned.1.call-update
  105.9 0.6 copy-done.1
  106.5 213.6 %all-reduce.2.cloned.1.call-done = f32[4096,128]{1,0:T(8,128)} async-done(((f32[4096,128]{1,0:T(8,128)}), f32[4096,128]{1,0:T(8,128)}) %all-reduce.2.cloned.1.call-update) | async-done | bytes 2097168 | tf_op jit(solution)/shard_map/psum | solution.py:60
  320.1 0.0 copy-start
  320.1 3.1 fusion.32
  323.2 0.0 copy-done
  323.2 1.5 fusion.31
  324.6 0.5 broadcast_multiply_fusion.1
  325.2 0.6 constant_dynamic-slice_fusion
  (36 shorter events, 0.3 us)
Async XLA Ops:
  7.2 312.9 %all-reduce.2.cloned.1.call-start = ((), (), s32[]{:S(2)}) async-start(), calls=%async_computation | async-start | bytes 4194304 | tf_op jit(solution)/shard_map/psum | solution.py:60
  105.8 0.7 copy-start.1
  320.1 3.1 copy-start
Sparse Core Ops, SparseCore 0:
  106.0 214.0 all-reduce.1
where the time goes:
time: 334 us; the launch traced here: 333 us
  waiting for transfers between devices  214 us (64%)
  matrix products  99 us (30%)
  between operations  14.1 us (4%)
  local copies, waits for them, and re-layouts  3.4 us (1%)
    psum x1, waiting for transfers between devices, per_device(): everything = lax.psum(running * scaling, 'blk')  214 us
    dot_general x16, matrix products, advance(): lax.dot_general(sign_tile, grad_block, (((0,), (1,)), ((), ())), preferre...  94.4 us
  transfers between devices with their start and end apart: 1, of which 1 were waited for; matrix products, arithmetic and copies ran while one was open for 0% of the time, Pallas kernels for 0%

commit v1 on v0

v1 whole, which is shorter than its diff:
```python
import functools
import math

import jax
import jax.numpy as jnp
from jax import lax
from jax.experimental import pallas as pl
from jax.experimental.pallas import tpu as pltpu
from jax.sharding import PartitionSpec as P

TILE = 512
PIECE = 16
WIDTH = 256
CORES = 2

golden_mult = -1640531535
mixer_one = -2048144789
mixer_two = -1028477387


def signs(table, seed):
    mixed = (table ^ seed) * jnp.int32(mixer_one)
    mixed = mixed ^ lax.shift_right_logical(mixed, jnp.int32(13))
    mixed = mixed * jnp.int32(mixer_two)
    mixed = mixed ^ lax.shift_right_logical(mixed, jnp.int32(16))
    return jnp.where(mixed.astype(jnp.int16) < 0, jnp.bfloat16(-1), jnp.bfloat16(1))


def project_kernel(own, half, units_ref, seeds_ref, grads_ref, out_ref, table):
    units = units_ref.shape[0]
    tiles = seeds_ref.shape[0]
    examples = grads_ref.shape[0]
    tile_rows = table.shape[0]
    unit_rows = half * tile_rows
    pieces = unit_rows // PIECE
    parts = TILE // WIDTH

    def run(*sums):
        acc = [sums[part * pieces : (part + 1) * pieces] for part in range(parts)]
        for part in range(parts):
            for one in acc[part]:
                pltpu.matmul_pop(one)

        def unit_step(unit, carry):
            x_parity, core, y_parity = units_ref[unit, 0], units_ref[unit, 1], units_ref[unit, 2]
            row = lax.broadcasted_iota(jnp.int32, table.shape, 0)
            param = lax.broadcasted_iota(jnp.int32, table.shape, 1)
            column = ((2 * (row // own) + x_parity) * CORES + core) * own + row % own
            product = (param * TILE + column) * jnp.int32(golden_mult)
            table[...] = product ^ lax.shift_right_logical(product, jnp.int32(16))

            def tile_step(tile, carry):
                for part in range(parts):
                    block = grads_ref[:, pl.ds(pl.multiple_of(tile * TILE + part * WIDTH, WIDTH), WIDTH)]
                    block = jnp.concatenate([block, jnp.zeros((WIDTH - examples, WIDTH), block.dtype)], axis=0)
                    pltpu.matmul_push_rhs(block, staging_register=0, mxu_index=part, transpose=True)
                for i in range(half):
                    seed = seeds_ref[tile, 2 * i + y_parity]
                    seed = seed ^ lax.shift_right_logical(seed, jnp.int32(16))
                    for start in range(0, tile_rows, PIECE):
                        piece = (i * tile_rows + start) // PIECE
                        for part in range(parts):
                            pltpu.matmul_acc_lhs(
                                acc[part][piece],
                                signs(table[start : start + PIECE, part * WIDTH : (part + 1) * WIDTH], seed),
                                load_staged_rhs=0 if piece == 0 else None,
                            )
                return carry

            lax.fori_loop(0, tiles, tile_step, 0)
            for piece in range(pieces):
                total = pltpu.matmul_pop(acc[0][piece])[:, :examples]
                for part in range(1, parts):
                    total = total + pltpu.matmul_pop(acc[part][piece])[:, :examples]
                out_ref[pl.ds(pl.multiple_of(unit * unit_rows + piece * PIECE, PIECE), PIECE), :] = total
            return carry

        lax.fori_loop(0, units, unit_step, 0)

    pl.run_scoped(run, *[pltpu.ACC(part)((PIECE, WIDTH), jnp.float32) for part in range(parts) for _ in range(pieces)])


def project(units, seeds, grads, own, side):
    examples, params = grads.shape
    half = side // 2
    tile_rows = half * own
    rows = units.shape[0] * half * tile_rows
    return pl.pallas_call(
        functools.partial(project_kernel, own, half),
        out_shape=jax.ShapeDtypeStruct((rows, examples), jnp.float32),
        in_specs=[
            pl.BlockSpec(memory_space=pltpu.SMEM),
            pl.BlockSpec(memory_space=pltpu.SMEM),
            pl.BlockSpec(memory_space=pltpu.VMEM),
        ],
        out_specs=pl.BlockSpec(memory_space=pltpu.VMEM),
        scratch_shapes=[pltpu.VMEM((tile_rows, TILE), jnp.int32)],
        compiler_params=pltpu.CompilerParams(vmem_limit_bytes=12 << 20),
        cost_estimate=pl.CostEstimate(
            flops=8 * rows * examples * params, bytes_accessed=2 * examples * params, transcendentals=0
        ),
        name="project",
    )(units, seeds, grads)


def finish_kernel(scaling, parts_ref, pairs_ref, own_ref, score_ref):
    total = parts_ref[0]
    for k in range(1, parts_ref.shape[0]):
        total = total + parts_ref[k]
    total = total * jnp.float32(scaling)
    own_ref[...] = total
    examples = total.shape[1]
    ids = lax.broadcasted_iota(jnp.int32, (examples, pairs_ref.shape[1]), 0)

    def pick(which):
        chosen = (ids == pairs_ref[which : which + 1, :]).astype(jnp.float32)
        return jnp.dot(total, chosen, precision=lax.Precision.HIGHEST, preferred_element_type=jnp.float32)

    score_ref[...] = jnp.sum(pick(0) * pick(1), axis=0, keepdims=True)


def finish(parts, pairs, scaling):
    vmem = pl.BlockSpec(memory_space=pltpu.VMEM)
    return pl.pallas_call(
        functools.partial(finish_kernel, scaling),
        out_shape=(
            jax.ShapeDtypeStruct(parts.shape[1:], jnp.float32),
            jax.ShapeDtypeStruct((1, pairs.shape[1]), jnp.float32),
        ),
        in_specs=[vmem, vmem],
        out_specs=(vmem, vmem),
        compiler_params=pltpu.CompilerParams(vmem_limit_bytes=12 << 20),
        name="finish",
    )(parts, pairs)


def per_device(example_grads, tile_seeds, pair_index):
    examples, params = example_grads.shape
    devices = lax.axis_size("blk")
    col_total = tile_seeds.shape[1] * TILE
    own = col_total // devices
    side = math.isqrt(devices // CORES)
    half = side // 2
    assert side * side * CORES == devices and side * CORES * own == TILE
    me = lax.axis_index("blk")
    core = me % CORES

    def place(y, x, c):
        return (y * side + x) * CORES + c

    order = [(px, py, i, j) for px in range(2) for py in range(2) for i in range(half) for j in range(half)]
    chips = [[place(2 * i + py, 2 * j + px, c) for px, py, i, j in order] for c in range(CORES)]
    partner = [(d, d ^ 1) for d in range(devices)]

    def units(which_core):
        return jnp.stack([jnp.stack([jnp.int32(px), which_core, jnp.int32(py)]) for px in range(2) for py in range(2)])

    theirs = project(units(1 - core), tile_seeds, example_grads, own, side)
    received = lax.ppermute(theirs, "blk", partner)
    mine = project(units(core), tile_seeds, example_grads, own, side)
    both = (mine + received).reshape(side * side, own, examples)
    parts = lax.all_to_all(both, "blk", 0, 0, axis_index_groups=chips, tiled=True)
    own_rows, partial = finish(parts, pair_index.T, 1.0 / math.sqrt(params * devices))
    partial = partial + lax.ppermute(partial, "blk", partner)
    spread = jnp.broadcast_to(partial[None], (side * side,) + partial.shape)
    shares = lax.all_to_all(spread, "blk", 0, 0, axis_index_groups=chips, tiled=True)
    scores = jnp.sum(shares, axis=(0, 1)) * (1.0 / math.sqrt(col_total))
    return (own_rows, scores)


def solution(mesh):
    placed = (P("grp", "blk"), P("blk", None), P("grp", None))
    return jax.shard_map(
        per_device,
        mesh=mesh,
        in_specs=placed,
        out_specs=(P("blk", "grp"), P("grp")),
        check_vma=False,
    )
```

time: 334 us -> 123 us (0.37)
  waiting for transfers between devices: 214 us -> 0.82 us
  matrix products: 99 us -> 0 us
  blocking collectives: 0 us -> 50.2 us
  Pallas kernels: 0 us -> 44.7 us
  starting transfers between devices: 0.06 us -> 22.6 us
  between operations: 14.1 us -> 0.71 us
    psum x1 -> x0, waiting for transfers between devices: 214 us -> none  [per_device(): everything = lax.psum(running * scaling, 'blk')]
    dot_general x18 -> x0, matrix products: 99 us -> none  [the longest x16 94.4 us: advance(): lax.dot_general(sign_tile, grad_block, (((0,), (1,)), ((), ())), preferre...]
    all_to_all x0 -> x2, blocking collectives: none -> 50.2 us  [the longest x1 34 us: per_device(): lax.all_to_all(both, 'blk', 0, 0, axis_index_groups=chips, tiled=True)]
    pallas_call x0 -> x3, Pallas kernels: none -> 44.7 us  [the longest x2 44 us: project(): pl.pallas_call(functools.partial(project_kernel, own, half), out_shape=ja...]
    ppermute x0 -> x2, starting transfers between devices: none -> 22.6 us  [the longest x1 20.5 us: per_device(): received = lax.ppermute(theirs, 'blk', partner)]
  transfers between devices with their start and end apart: 1 -> 2, of which waited for: 1 -> 1; matrix products, arithmetic and copies ran while one was open for 0% -> 0% of each run, Pallas kernels for 0% -> 18%
where the time goes in v1:
time: 123 us; the launch traced here: 122 us
  blocking collectives  50.2 us (41%)
  Pallas kernels  44.7 us (36%)
  starting transfers between devices  22.6 us (18%)
  local copies, waits for them, and re-layouts  2.38 us (2%)
    pallas_call x2, Pallas kernels, project(): pl.pallas_call(functools.partial(project_kernel, own, half), out_shape=ja...  44 us
    all_to_all x1, blocking collectives, per_device(): lax.all_to_all(both, 'blk', 0, 0, axis_index_groups=chips, tiled=True)  34 us
    ppermute x1, starting transfers between devices, per_device(): received = lax.ppermute(theirs, 'blk', partner)  20.5 us
    all_to_all x1, blocking collectives, per_device(): lax.all_to_all(spread, 'blk', 0, 0, axis_index_groups=chips, tiled=True)  16.2 us
  transfers between devices with their start and end apart: 2, of which 1 were waited for; matrix products, arithmetic and copies ran while one was open for 0% of the time, Pallas kernels for 18%

profile of v1, /device:TPU:513, one launch (start us, length us, event | category | flops | bytes accessed | tf_op | source)
XLA Modules:
  0.0 122.4 jit_solution(15665621476377485204)
XLA Ops:
  0.6 0.1 fusion.4
  0.7 0.1 fusion.5
  0.8 0.1 fusion.2
  0.9 0.8 copy.9.seeds_ref
  1.6 0.0 copy-start.1
  1.7 1.6 %copy-done.1 = bf16[128,8192]{1,0:T(8,128)(2,1)S(1)} copy-done((bf16[128,8192]{1,0:T(8,128)(2,1)S(1)}, bf16[128,8192]{1,0:T(8,128)(2,1)}, u32[]{:S(2)}) %copy-start.1) | copy-done | bytes 2097176
  3.2 0.0 copy-start.2
  3.2 22.0 %project.3 = f32[2048,128]{1,0:T(8,128)S(1)} custom-call(s32[4,3]{1,0:T(4,128)S(1)} %pad_add_fusion.1.units_ref, s32[16,8]{1,0:T(8,128)S(1)} %copy.9.seeds_ref, bf16[128,8192]{1,0:T(8,128)(2,1)S(1)} %copy-done.1), custom_call_target="tpu_custom_call" | custom-call | flops 17179869184 | bytes 2097152 | tf_op jit(solution)/shard_map/project/pallas_call | solution.py:88
  25.2 20.5 %collective-permute-start = (f32[2048,128]{1,0:T(8,128)S(1)}, f32[2048,128]{1,0:T(8,128)S(1)}, u32[]{:S(2)}, u32[]{:S(2)}) collective-permute-start(f32[2048,128]{1,0:T(8,128)S(1)} %project.3), channel_id=1, source_target_pairs={{0,1},{1,0},{2,3},{3,2},{4,5},{5,4},{6,7},{7,6},{8,9},{9,8},{10,11... | collective-permute-start | bytes 3145736 | tf_op jit(solution)/shard_map/ppermute | solution.py:159
  45.8 0.1 fusion
  45.9 0.0 copy-done.2
  45.9 22.0 %project.2 = f32[2048,128]{1,0:T(8,128)S(1)} custom-call(s32[4,3]{1,0:T(4,128)S(1)} %pad_add_fusion.units_ref, s32[16,8]{1,0:T(8,128)S(1)} %copy.9.seeds_ref, bf16[128,8192]{1,0:T(8,128)(2,1)S(1)} %copy-done.2), custom_call_target="tpu_custom_call" | custom-call | flops 17179869184 | bytes 2097152 | tf_op jit(solution)/shard_map/project/pallas_call | solution.py:88
  67.8 0.0 copy-start
  67.9 0.0 collective-permute-done
  67.9 0.1 add.11
  68.0 34.0 %all_to_all.10.parts_ref = f32[64,32,128]{2,1,0:T(8,128)S(1)} all-to-all(f32[64,32,128]{2,1,0:T(8,128)S(1)} %bitcast.24), channel_id=1, replica_groups={{0,4,8,12,32,36,40,44,64,68,72,76,96,100,104,108,16,20,24,28,48,52,56,6..., dimensions={0} | all-to-all | bytes 2097152 | tf_op jit(solution)/shard_map/all_to_all | solution.py:162
  102.0 0.0 copy-done
  102.0 0.7 finish.1
  102.7 2.1 %collective-permute-start.1 = (f32[1,64]{1,0:T(1,128)S(1)}, f32[1,64]{1,0:T(1,128)S(1)}, u32[]{:S(2)}, u32[]{:S(2)}) collective-permute-start(f32[1,64]{1,0:T(1,128)S(1)} %get-tuple-element.5), channel_id=1, source_target_pairs={{0,1},{1,0},{2,3},{3,2},{4,5},{5,4},{6,7},{7,6},{8,9},{9,8},{10,11... | collective-permute-start | bytes 776 | tf_op jit(solution)/shard_map/ppermute | solution.py:164
  104.8 0.8 collective-permute-done.1
  105.6 16.2 %all_to_all.11 = f32[64,1,64]{2,1,0:T(1,128)S(1)} all-to-all(f32[64,1,64]{2,1,0:T(1,128)S(1)} %broadcast_in_dim.9), channel_id=1, replica_groups={{0,4,8,12,32,36,40,44,64,68,72,76,96,100,104,108,16,20,24,28,48,52,56,6..., dimensions={0} | all-to-all | bytes 32768 | tf_op jit(solution)/shard_map/all_to_all | solution.py:166
  121.8 0.5 broadcast_multiply_fusion
  (5 shorter events, 0.1 us)
Async XLA Ops:
  1.6 1.6 %copy-start.1 = (bf16[128,8192]{1,0:T(8,128)(2,1)S(1)}, bf16[128,8192]{1,0:T(8,128)(2,1)}, u32[]{:S(2)}) copy-start(bf16[128,8192]{1,0:T(8,128)(2,1)} %grads_ref.3) | copy-start | bytes 6291460
  3.2 42.6 %copy-start.2 = (bf16[128,8192]{1,0:T(8,128)(2,1)S(1)}, bf16[128,8192]{1,0:T(8,128)(2,1)}, u32[]{:S(2)}) copy-start(bf16[128,8192]{1,0:T(8,128)(2,1)} %grads_ref.3) | copy-start | bytes 6291460
  25.2 42.6 %collective-permute-start = (f32[2048,128]{1,0:T(8,128)S(1)}, f32[2048,128]{1,0:T(8,128)S(1)}, u32[]{:S(2)}, u32[]{:S(2)}) collective-permute-start(f32[2048,128]{1,0:T(8,128)S(1)} %project.3), channel_id=1, source_target_pairs={{0,1},{1,0},{2,3},{3,2},{4,5},{5,4},{6,7},{7,6},{8,9},{9,8},{10,11... | collective-permute-start | bytes 3145736 | tf_op jit(solution)/shard_map/ppermute | solution.py:159
  67.8 34.2 %copy-start = (s32[64,2]{0,1:T(2,128)S(1)}, s32[64,2]{0,1:T(2,128)}, u32[]{:S(2)}) copy-start(s32[64,2]{0,1:T(2,128)} %param.5) | copy-start | bytes 1540
  102.7 2.9 %collective-permute-start.1 = (f32[1,64]{1,0:T(1,128)S(1)}, f32[1,64]{1,0:T(1,128)S(1)}, u32[]{:S(2)}, u32[]{:S(2)}) collective-permute-start(f32[1,64]{1,0:T(1,128)S(1)} %get-tuple-element.5), channel_id=1, source_target_pairs={{0,1},{1,0},{2,3},{3,2},{4,5},{5,4},{6,7},{7,6},{8,9},{9,8},{10,11... | collective-permute-start | bytes 776 | tf_op jit(solution)/shard_map/ppermute | solution.py:164

commit v2 on v1

--- a/solution.py
+++ b/solution.py
@@ -26,8 +26,13 @@
     return jnp.where(mixed.astype(jnp.int16) < 0, jnp.bfloat16(-1), jnp.bfloat16(1))
 
 
-def project_kernel(own, half, units_ref, seeds_ref, grads_ref, out_ref, table):
-    units = units_ref.shape[0]
+def project_kernel(own, half, side, units, flips, me_ref, seeds_ref, grads_ref, out_ref, table):
+    me = me_ref[0]
+    own_core = me & (CORES - 1)
+    own_x = (me // CORES) & 1
+    own_y = (me // (CORES * side)) & 1
+    x_flip, y_flip, core_flip = flips
+    x_parity, core = own_x ^ x_flip, own_core ^ core_flip
     tiles = seeds_ref.shape[0]
     examples = grads_ref.shape[0]
     tile_rows = table.shape[0]
@@ -41,14 +46,14 @@
             for one in acc[part]:
                 pltpu.matmul_pop(one)
 
+        row = lax.broadcasted_iota(jnp.int32, table.shape, 0)
+        param = lax.broadcasted_iota(jnp.int32, table.shape, 1)
+        column = ((2 * (row // own) + x_parity) * CORES + core) * own + row % own
+        product = (param * TILE + column) * jnp.int32(golden_mult)
+        table[...] = product ^ lax.shift_right_logical(product, jnp.int32(16))
+
         def unit_step(unit, carry):
-            x_parity, core, y_parity = units_ref[unit, 0], units_ref[unit, 1], units_ref[unit, 2]
-            row = lax.broadcasted_iota(jnp.int32, table.shape, 0)
-            param = lax.broadcasted_iota(jnp.int32, table.shape, 1)
-            column = ((2 * (row // own) + x_parity) * CORES + core) * own + row % own
-            product = (param * TILE + column) * jnp.int32(golden_mult)
-            table[...] = product ^ lax.shift_right_logical(product, jnp.int32(16))
-
+            y_parity = own_y ^ y_flip ^ (unit & 1)
             def tile_step(tile, carry):
                 for part in range(parts):
                     block = grads_ref[:, pl.ds(pl.multiple_of(tile * TILE + part * WIDTH, WIDTH), WIDTH)]
@@ -80,13 +85,13 @@
     pl.run_scoped(run, *[pltpu.ACC(part)((PIECE, WIDTH), jnp.float32) for part in range(parts) for _ in range(pieces)])
 
 
-def project(units, seeds, grads, own, side):
+def project(me, seeds, grads, own, side, units, flips):
     examples, params = grads.shape
     half = side // 2
     tile_rows = half * own
-    rows = units.shape[0] * half * tile_rows
+    rows = units * half * tile_rows
     return pl.pallas_call(
-        functools.partial(project_kernel, own, half),
+        functools.partial(project_kernel, own, half, side, units, flips),
         out_shape=jax.ShapeDtypeStruct((rows, examples), jnp.float32),
         in_specs=[
             pl.BlockSpec(memory_space=pltpu.SMEM),
@@ -100,7 +105,7 @@
             flops=8 * rows * examples * params, bytes_accessed=2 * examples * params, transcendentals=0
         ),
         name="project",
-    )(units, seeds, grads)
+    )(me, seeds, grads)
 
 
 def finish_kernel(scaling, parts_ref, pairs_ref, own_ref, score_ref):
@@ -141,27 +146,36 @@
     own = col_total // devices
     side = math.isqrt(devices // CORES)
     half = side // 2
-    assert side * side * CORES == devices and side * CORES * own == TILE
-    me = lax.axis_index("blk")
-    core = me % CORES
+    assert side * side * CORES == devices and side * CORES * own == TILE and side % 2 == 0
+    me = lax.axis_index("blk").astype(jnp.int32).reshape(1)
 
     def place(y, x, c):
         return (y * side + x) * CORES + c
 
-    order = [(px, py, i, j) for px in range(2) for py in range(2) for i in range(half) for j in range(half)]
-    chips = [[place(2 * i + py, 2 * j + px, c) for px, py, i, j in order] for c in range(CORES)]
-    partner = [(d, d ^ 1) for d in range(devices)]
+    def swap(array, flip):
+        return lax.ppermute(array, "blk", [(d, d ^ flip) for d in range(devices)])
 
-    def units(which_core):
-        return jnp.stack([jnp.stack([jnp.int32(px), which_core, jnp.int32(py)]) for px in range(2) for py in range(2)])
+    def columns(units, x_flip, y_flip, core_flip):
+        return project(me, tile_seeds, example_grads, own, side, units, (x_flip, y_flip, core_flip))
 
-    theirs = project(units(1 - core), tile_seeds, example_grads, own, side)
-    received = lax.ppermute(theirs, "blk", partner)
-    mine = project(units(core), tile_seeds, example_grads, own, side)
-    both = (mine + received).reshape(side * side, own, examples)
-    parts = lax.all_to_all(both, "blk", 0, 0, axis_index_groups=chips, tiled=True)
+    alike = [
+        [place(2 * i + py, 2 * j + px, c) for i in range(half) for j in range(half)]
+        for py in range(2)
+        for px in range(2)
+        for c in range(CORES)
+    ]
+    chips = [[place(y, x, c) for y in range(side) for x in range(side)] for c in range(CORES)]
+    next_core, next_x, next_y = 1, CORES, CORES * side
+    middle = half * half * own
+
+    other_x = swap(columns(2, 1, 1, 1), next_core) + columns(2, 1, 1, 0)
+    other_x = swap(other_x, next_x)
+    other_y = swap(columns(1, 0, 1, 1), next_core) + columns(1, 0, 1, 0) + other_x[:middle]
+    other_y = swap(other_y, next_y)
+    same = swap(columns(1, 0, 0, 1), next_core) + columns(1, 0, 0, 0) + other_x[middle:] + other_y
+    parts = lax.all_to_all(same.reshape(half * half, own, examples), "blk", 0, 0, axis_index_groups=alike, tiled=True)
     own_rows, partial = finish(parts, pair_index.T, 1.0 / math.sqrt(params * devices))
-    partial = partial + lax.ppermute(partial, "blk", partner)
+    partial = partial + swap(partial, next_core)
     spread = jnp.broadcast_to(partial[None], (side * side,) + partial.shape)
     shares = lax.all_to_all(spread, "blk", 0, 0, axis_index_groups=chips, tiled=True)
     scores = jnp.sum(shares, axis=(0, 1)) * (1.0 / math.sqrt(col_total))

time: 123 us -> 110 us (0.89)
  blocking collectives: 50.2 us -> 32.5 us
  Pallas kernels: 44.7 us -> 47.1 us
  starting transfers between devices: 22.6 us -> 24.9 us
    all_to_all x1, blocking collectives: 34 us -> 15.2 us  [per_device(): lax.all_to_all(same.reshape(half * half, own, examples), 'blk', 0, 0, axi...]
    pallas_call x2 -> x6, Pallas kernels: 44 us -> 46.4 us  [project(): pl.pallas_call(functools.partial(project_kernel, own, half, side, units,...]
    ppermute x2 -> x6, starting transfers between devices: 22.6 us -> 24.9 us  [swap(): return lax.ppermute(array, 'blk', [(d, d ^ flip) for d in range(devices)])]
  transfers between devices with their start and end apart: 2 -> 6, of which waited for: 1 -> 3; matrix products, arithmetic and copies ran while one was open for 0% -> 0% of each run, Pallas kernels for 18% -> 32%
where the time goes in v2:
time: 110 us
  Pallas kernels  47.1 us (43%)
  blocking collectives  32.5 us (30%)
  starting transfers between devices  24.9 us (23%)
  local copies, waits for them, and re-layouts  2.38 us (2%)
  waiting for transfers between devices  1.69 us (2%)
    pallas_call x6, Pallas kernels, project(): pl.pallas_call(functools.partial(project_kernel, own, half, side, units,...  46.4 us
    ppermute x6, starting transfers between devices, swap(): return lax.ppermute(array, 'blk', [(d, d ^ flip) for d in range(devices)])  24.9 us
    all_to_all x1, blocking collectives, per_device(): lax.all_to_all(spread, 'blk', 0, 0, axis_index_groups=chips, tiled=True)  17.3 us
    all_to_all x1, blocking collectives, per_device(): lax.all_to_all(same.reshape(half * half, own, examples), 'blk', 0, 0, axi...  15.2 us
    unnamed x7, local copies, waits for them, and re-layouts  2.36 us
  transfers between devices with their start and end apart: 6, of which 3 were waited for; matrix products, arithmetic and copies ran while one was open for 0% of the time, Pallas kernels for 32%

profile of v2, /device:TPU:513, one launch (start us, length us, event | category | flops | bytes accessed | tf_op | source)
XLA Modules:
  0.0 110.0 jit_solution(4844081953985441334)
XLA Ops:
  0.6 0.8 copy.17.seeds_ref
  1.4 0.0 copy-start.1
  1.4 1.6 %copy-done.1 = bf16[128,8192]{1,0:T(8,128)(2,1)S(1)} copy-done((bf16[128,8192]{1,0:T(8,128)(2,1)S(1)}, bf16[128,8192]{1,0:T(8,128)(2,1)}, u32[]{:S(2)}) %copy-start.1) | copy-done | bytes 2097176
  3.0 11.2 %project.8 = f32[1024,128]{1,0:T(8,128)S(1)} custom-call(s32[1]{0:T(128)} %bitcast.me_ref, s32[16,8]{1,0:T(8,128)S(1)} %copy.17.seeds_ref, bf16[128,8192]{1,0:T(8,128)(2,1)S(1)} %copy-done.1), custom_call_target="tpu_custom_call" | custom-call | flops 8589934592 | bytes 2097152 | tf_op jit(solution)/shard_map/project/pallas_call | solution.py:93
  14.2 20.5 %collective-permute-start.1 = (f32[1024,128]{1,0:T(8,128)S(1)}, f32[1024,128]{1,0:T(8,128)S(1)}, u32[]{:S(2)}, u32[]{:S(2)}) collective-permute-start(f32[1024,128]{1,0:T(8,128)S(1)} %project.8), channel_id=1, source_target_pairs={{0,1},{1,0},{2,3},{3,2},{4,5},{5,4},{6,7},{7,6},{8,9},{9,8},{10,11... | collective-permute-start | bytes 1572872 | tf_op jit(solution)/shard_map/ppermute | solution.py:156
  34.8 6.0 %project.10 = f32[512,128]{1,0:T(8,128)S(1)} custom-call(s32[1]{0:T(128)} %bitcast.me_ref, s32[16,8]{1,0:T(8,128)S(1)} %copy.17.seeds_ref, bf16[128,8192]{1,0:T(8,128)(2,1)S(1)} %copy-done.1), custom_call_target="tpu_custom_call" | custom-call | flops 4294967296 | bytes 2097152 | tf_op jit(solution)/shard_map/project/pallas_call | solution.py:93
  40.7 0.0 copy-start.2
  40.8 0.1 collective-permute-start.3
  40.9 11.2 %project.9 = f32[1024,128]{1,0:T(8,128)S(1)} custom-call(s32[1]{0:T(128)} %bitcast.me_ref, s32[16,8]{1,0:T(8,128)S(1)} %copy.17.seeds_ref, bf16[128,8192]{1,0:T(8,128)(2,1)S(1)} %copy-done.1), custom_call_target="tpu_custom_call" | custom-call | flops 8589934592 | bytes 2097152 | tf_op jit(solution)/shard_map/project/pallas_call | solution.py:93
  52.1 0.0 collective-permute-done.1
  52.2 0.1 add.22
  52.2 0.1 collective-permute-start.2
  52.4 0.0 copy-done.2
  52.4 6.0 %project.6 = f32[512,128]{1,0:T(8,128)S(1)} custom-call(s32[1]{0:T(128)} %bitcast.me_ref, s32[16,8]{1,0:T(8,128)S(1)} %copy.17.seeds_ref, bf16[128,8192]{1,0:T(8,128)(2,1)S(1)} %copy-done.2), custom_call_target="tpu_custom_call" | custom-call | flops 4294967296 | bytes 2097152 | tf_op jit(solution)/shard_map/project/pallas_call | solution.py:93
  58.4 0.6 collective-permute-start
  59.0 6.0 %project.11 = f32[512,128]{1,0:T(8,128)S(1)} custom-call(s32[1]{0:T(128)} %bitcast.me_ref, s32[16,8]{1,0:T(8,128)S(1)} %copy.17.seeds_ref, bf16[128,8192]{1,0:T(8,128)(2,1)S(1)} %copy-done.2), custom_call_target="tpu_custom_call" | custom-call | flops 4294967296 | bytes 2097152 | tf_op jit(solution)/shard_map/project/pallas_call | solution.py:93
  65.0 0.0 collective-permute-done.3
  65.0 0.4 collective-permute-done.2
  65.3 0.1 slice_add_fusion
  65.4 0.0 copy-start
  65.4 0.1 collective-permute-start.4
  65.6 6.0 %project.7 = f32[512,128]{1,0:T(8,128)S(1)} custom-call(s32[1]{0:T(128)} %bitcast.me_ref, s32[16,8]{1,0:T(8,128)S(1)} %copy.17.seeds_ref, bf16[128,8192]{1,0:T(8,128)(2,1)S(1)} %copy-done.2), custom_call_target="tpu_custom_call" | custom-call | flops 4294967296 | bytes 2097152 | tf_op jit(solution)/shard_map/project/pallas_call | solution.py:93
  71.5 0.0 collective-permute-done
  71.6 0.5 collective-permute-done.4
  72.1 0.1 fusion
  72.1 15.2 %all_to_all.10.parts_ref = f32[16,32,128]{2,1,0:T(8,128)S(1)} all-to-all(f32[16,32,128]{2,1,0:T(8,128)S(1)} %bitcast.7), channel_id=1, replica_groups={{0,4,8,12,32,36,40,44,64,68,72,76,96,100,104,108},{1,5,9,13,33,37,41,45..., dimensions={0} | all-to-all | bytes 524288 | tf_op jit(solution)/shard_map/all_to_all | solution.py:176
  87.3 0.0 copy-done
  87.3 0.7 finish.1
  88.0 3.3 %collective-permute-start.5 = (f32[1,64]{1,0:T(1,128)S(1)}, f32[1,64]{1,0:T(1,128)S(1)}, u32[]{:S(2)}, u32[]{:S(2)}) collective-permute-start(f32[1,64]{1,0:T(1,128)S(1)} %get-tuple-element.5), channel_id=1, source_target_pairs={{0,1},{1,0},{2,3},{3,2},{4,5},{5,4},{6,7},{7,6},{8,9},{9,8},{10,11... | collective-permute-start | bytes 776 | tf_op jit(solution)/shard_map/ppermute | solution.py:156
  91.3 0.8 collective-permute-done.5
  92.2 17.3 %all_to_all.11 = f32[64,1,64]{2,1,0:T(1,128)S(1)} all-to-all(f32[64,1,64]{2,1,0:T(1,128)S(1)} %broadcast_in_dim.9), channel_id=1, replica_groups={{0,2,4,6,8,10,12,14,16,18,20,22,24,26,28,30,32,34,36,38,40,42,44,46,48,..., dimensions={0} | all-to-all | bytes 32768 | tf_op jit(solution)/shard_map/all_to_all | solution.py:180
  109.5 0.5 broadcast_multiply_fusion
  (3 shorter events, 0.1 us)
Async XLA Ops:
  1.4 1.6 %copy-start.1 = (bf16[128,8192]{1,0:T(8,128)(2,1)S(1)}, bf16[128,8192]{1,0:T(8,128)(2,1)}, u32[]{:S(2)}) copy-start(bf16[128,8192]{1,0:T(8,128)(2,1)} %grads_ref.11) | copy-start | bytes 6291460
  14.2 37.9 %collective-permute-start.1 = (f32[1024,128]{1,0:T(8,128)S(1)}, f32[1024,128]{1,0:T(8,128)S(1)}, u32[]{:S(2)}, u32[]{:S(2)}) collective-permute-start(f32[1024,128]{1,0:T(8,128)S(1)} %project.8), channel_id=1, source_target_pairs={{0,1},{1,0},{2,3},{3,2},{4,5},{5,4},{6,7},{7,6},{8,9},{9,8},{10,11... | collective-permute-start | bytes 1572872 | tf_op jit(solution)/shard_map/ppermute | solution.py:156
  40.7 11.6 %copy-start.2 = (bf16[128,8192]{1,0:T(8,128)(2,1)S(1)}, bf16[128,8192]{1,0:T(8,128)(2,1)}, u32[]{:S(2)}) copy-start(bf16[128,8192]{1,0:T(8,128)(2,1)} %grads_ref.11) | copy-start | bytes 6291460
  40.8 24.2 %collective-permute-start.3 = (f32[512,128]{1,0:T(8,128)S(1)}, f32[512,128]{1,0:T(8,128)S(1)}, u32[]{:S(2)}, u32[]{:S(2)}) collective-permute-start(f32[512,128]{1,0:T(8,128)S(1)} %project.10), channel_id=1, source_target_pairs={{0,1},{1,0},{2,3},{3,2},{4,5},{5,4},{6,7},{7,6},{8,9},{9,8},{10,11... | collective-permute-start | bytes 786440 | tf_op jit(solution)/shard_map/ppermute | solution.py:156
  52.2 13.1 %collective-permute-start.2 = (f32[1024,128]{1,0:T(8,128)S(1)}, f32[1024,128]{1,0:T(8,128)S(1)}, u32[]{:S(2)}, u32[]{:S(2)}) collective-permute-start(f32[1024,128]{1,0:T(8,128)S(1)} %add.22), channel_id=1, source_target_pairs={{0,2},{1,3},{2,0},{3,1},{4,6},{5,7},{6,4},{7,5},{8,10},{9,11},{10,... | collective-permute-start | bytes 1572872 | tf_op jit(solution)/shard_map/ppermute | solution.py:156
  58.4 13.2 %collective-permute-start = (f32[512,128]{1,0:T(8,128)S(1)}, f32[512,128]{1,0:T(8,128)S(1)}, u32[]{:S(2)}, u32[]{:S(2)}) collective-permute-start(f32[512,128]{1,0:T(8,128)S(1)} %project.6), channel_id=1, source_target_pairs={{0,1},{1,0},{2,3},{3,2},{4,5},{5,4},{6,7},{7,6},{8,9},{9,8},{10,11... | collective-permute-start | bytes 786440 | tf_op jit(solution)/shard_map/ppermute | solution.py:156
  65.4 21.9 %copy-start = (s32[64,2]{0,1:T(2,128)S(1)}, s32[64,2]{0,1:T(2,128)}, u32[]{:S(2)}) copy-start(s32[64,2]{0,1:T(2,128)} %param.5) | copy-start | bytes 1540
  65.4 6.6 %collective-permute-start.4 = (f32[512,128]{1,0:T(8,128)S(1)}, f32[512,128]{1,0:T(8,128)S(1)}, u32[]{:S(2)}, u32[]{:S(2)}) collective-permute-start(f32[512,128]{1,0:T(8,128)S(1)} %slice_add_fusion), channel_id=1, source_target_pairs={{0,16},{1,17},{2,18},{3,19},{4,20},{5,21},{6,22},{7,23},{8,24},{9,... | collective-permute-start | bytes 786440 | tf_op jit(solution)/shard_map/ppermute | solution.py:156
  88.0 4.1 %collective-permute-start.5 = (f32[1,64]{1,0:T(1,128)S(1)}, f32[1,64]{1,0:T(1,128)S(1)}, u32[]{:S(2)}, u32[]{:S(2)}) collective-permute-start(f32[1,64]{1,0:T(1,128)S(1)} %get-tuple-element.5), channel_id=1, source_target_pairs={{0,1},{1,0},{2,3},{3,2},{4,5},{5,4},{6,7},{7,6},{8,9},{9,8},{10,11... | collective-permute-start | bytes 776 | tf_op jit(solution)/shard_map/ppermute | solution.py:156

commit v3 on v2

v3 whole, which is shorter than its diff:
```python
import functools
import math

import jax
import jax.numpy as jnp
from jax import lax
from jax.experimental import pallas as pl
from jax.experimental.pallas import tpu as pltpu
from jax.sharding import PartitionSpec as P


TILE = 512
PIECE = 16
WIDTH = 256
CORES = 2

golden_mult = -1640531535
mixer_one = -2048144789
mixer_two = -1028477387


def signs(table, seed):
    mixed = (table ^ seed) * jnp.int32(mixer_one)
    mixed = mixed ^ lax.shift_right_logical(mixed, jnp.int32(13))
    mixed = mixed * jnp.int32(mixer_two)
    mixed = mixed ^ lax.shift_right_logical(mixed, jnp.int32(16))
    return jnp.where(mixed.astype(jnp.int16) < 0, jnp.bfloat16(-1), jnp.bfloat16(1))


def prepare_kernel(half, side, me_ref, seeds_ref, rows_ref):
    tiles = seeds_ref.shape[0]
    me = me_ref[0]
    own_y = (me // (CORES * side)) & 1
    last = 2 * half * tiles
    rows_ref[last:, :] = jnp.full((rows_ref.shape[0] - last, WIDTH), me & (2 * CORES - 1), jnp.int32)
    seeds = seeds_ref[...]
    seeds = seeds ^ lax.shift_right_logical(seeds, jnp.int32(16))
    for y in range(2 * half):
        row = pl.multiple_of((((y & 1) ^ own_y) * half + y // 2) * tiles, tiles)
        rows_ref[pl.ds(row, tiles), :] = jnp.broadcast_to(seeds[:, y : y + 1], (tiles, WIDTH))


def prepare(me, seeds, side):
    half = side // 2
    vmem = pl.BlockSpec(memory_space=pltpu.VMEM)
    return pl.pallas_call(
        functools.partial(prepare_kernel, half, side),
        out_shape=jax.ShapeDtypeStruct((2 * seeds.shape[0] * half + 8, WIDTH), jnp.int32),
        in_specs=[pl.BlockSpec(memory_space=pltpu.SMEM), vmem],
        out_specs=vmem,
        compiler_params=pltpu.CompilerParams(vmem_limit_bytes=12 << 20),
        cost_estimate=pl.CostEstimate(flops=1 << 30, bytes_accessed=1 << 16, transcendentals=0),
        name="prepare",
    )(me, seeds)


def project_kernel(own, half, tiles, flips, after_ref, seeds_ref, grads_ref, out_ref, table):
    del after_ref
    x_flip, y_flip, core_flip = flips
    examples = grads_ref.shape[0]
    tile_rows = table.shape[0]
    unit_rows = half * tile_rows
    pieces = unit_rows // PIECE
    parts = TILE // WIDTH

    def run(*sums):
        acc = [sums[part * pieces : (part + 1) * pieces] for part in range(parts)]
        for part in range(parts):
            for one in acc[part]:
                pltpu.matmul_pop(one)
        place = seeds_ref[2 * tiles * half : 2 * tiles * half + 1, :] ^ (x_flip * CORES + core_flip)
        row = lax.broadcasted_iota(jnp.int32, (tile_rows, WIDTH), 0)
        column = (row // own) * (2 * CORES * own) + row % own + place * own
        for start in range(0, TILE, WIDTH):
            param = lax.broadcasted_iota(jnp.int32, (tile_rows, WIDTH), 1) + start
            product = (param * TILE + column) * jnp.int32(golden_mult)
            table[:, start : start + WIDTH] = product ^ lax.shift_right_logical(product, jnp.int32(16))

        def push(tile):
            for part in range(parts):
                block = grads_ref[:, pl.ds(pl.multiple_of(tile * TILE + part * WIDTH, WIDTH), WIDTH)]
                block = jnp.concatenate([block, jnp.zeros((WIDTH - examples, WIDTH), block.dtype)], axis=0)
                pltpu.matmul_push_rhs(block, staging_register=0, mxu_index=part, transpose=True)

        def tile_step(first_seed, tile, following):
            for i in range(half):
                seed = seeds_ref[pl.ds(first_seed + i * tiles + tile, 1), :]
                for start in range(0, tile_rows, PIECE):
                    piece = (i * tile_rows + start) // PIECE
                    for part in range(parts):
                        pltpu.matmul_acc_lhs(
                            acc[part][piece],
                            signs(table[start : start + PIECE, part * WIDTH : (part + 1) * WIDTH], seed),
                            load_staged_rhs=0 if piece == 0 else None,
                        )
                    if piece == 0 and following is not None:
                        push(following)

        first_seed = y_flip * half * tiles
        push(0)

        def pair_step(pair, carry):
            tile_step(first_seed, 2 * pair, 2 * pair + 1)
            tile_step(first_seed, 2 * pair + 1, 2 * pair + 2)
            return carry

        lax.fori_loop(0, tiles // 2 - 1, pair_step, 0)
        tile_step(first_seed, tiles - 2, tiles - 1)
        tile_step(first_seed, tiles - 1, None)
        for piece in range(pieces):
            total = pltpu.matmul_pop(acc[0][piece])[:, :examples]
            for part in range(1, parts):
                total = total + pltpu.matmul_pop(acc[part][piece])[:, :examples]
            out_ref[piece * PIECE : (piece + 1) * PIECE, :] = total

    pl.run_scoped(run, *[pltpu.ACC(part)((PIECE, WIDTH), jnp.float32) for part in range(parts) for _ in range(pieces)])


def project(after, seeds, grads, own, side, flips):
    examples, params = grads.shape
    half = side // 2
    tile_rows = half * own
    rows = half * tile_rows
    vmem = pl.BlockSpec(memory_space=pltpu.VMEM)
    return pl.pallas_call(
        functools.partial(project_kernel, own, half, params // TILE, flips),
        out_shape=jax.ShapeDtypeStruct((rows, examples), jnp.float32),
        in_specs=[vmem, vmem, vmem],
        out_specs=vmem,
        scratch_shapes=[pltpu.VMEM((tile_rows, TILE), jnp.int32)],
        compiler_params=pltpu.CompilerParams(vmem_limit_bytes=12 << 20),
        cost_estimate=pl.CostEstimate(
            flops=8 * rows * examples * params, bytes_accessed=2 * examples * params, transcendentals=0
        ),
        name="project",
    )(after, seeds, grads)


def finish_kernel(scaling, score_scaling, parts_ref, pairs_ref, own_ref, score_ref):
    total = parts_ref[0]
    for k in range(1, parts_ref.shape[0]):
        total = total + parts_ref[k]
    total = total * jnp.float32(scaling)
    own_ref[...] = total
    examples = total.shape[1]
    ids = lax.broadcasted_iota(jnp.int32, (examples, pairs_ref.shape[1]), 0)

    def pick(which):
        chosen = (ids == pairs_ref[which : which + 1, :]).astype(jnp.float32)
        return jnp.dot(total, chosen, precision=lax.Precision.HIGHEST, preferred_element_type=jnp.float32)

    score_ref[...] = jnp.sum(pick(0) * pick(1), axis=0, keepdims=True) * jnp.float32(score_scaling)


def finish(parts, pairs, scaling, score_scaling):
    vmem = pl.BlockSpec(memory_space=pltpu.VMEM)
    return pl.pallas_call(
        functools.partial(finish_kernel, scaling, score_scaling),
        out_shape=(
            jax.ShapeDtypeStruct(parts.shape[1:], jnp.float32),
            jax.ShapeDtypeStruct((1, pairs.shape[1]), jnp.float32),
        ),
        in_specs=[vmem, vmem],
        out_specs=(vmem, vmem),
        compiler_params=pltpu.CompilerParams(vmem_limit_bytes=12 << 20),
        name="finish",
    )(parts, pairs)


def per_device(example_grads, tile_seeds, pair_index):
    examples, params = example_grads.shape
    devices = lax.axis_size("blk")
    col_total = tile_seeds.shape[1] * TILE
    own = col_total // devices
    side = math.isqrt(devices // CORES)
    half = side // 2
    assert side * side * CORES == devices and side * CORES * own == TILE and side % 2 == 0
    me = lax.axis_index("blk").astype(jnp.int32).reshape(1)

    def place(y, x, c):
        return (y * side + x) * CORES + c

    def swap(array, flip):
        return lax.ppermute(array, "blk", [(d, d ^ flip) for d in range(devices)])

    seeds = prepare(me, tile_seeds, side)

    alike = [
        [place(2 * i + py, 2 * j + px, c) for i in range(half) for j in range(half)]
        for py in range(2)
        for px in range(2)
        for c in range(CORES)
    ]
    chips = [[place(y, x, c) for y in range(side) for x in range(side)] for c in range(CORES)]
    next_core, next_x, next_y = 1, CORES, CORES * side

    def columns(after, x_flip, y_flip, core_flip):
        return project(after, seeds, example_grads, own, side, (x_flip, y_flip, core_flip))

    both_far = columns(seeds, 1, 1, 1)
    x_far = columns(both_far, 1, 0, 1)
    both = columns(x_far, 1, 1, 0) + swap(both_far, next_core)
    both_in = swap(both, next_x)
    x_own = columns(both, 1, 0, 0) + swap(x_far, next_core)
    x_in = swap(x_own, next_x)
    y_far = columns(x_own, 0, 1, 1)
    y_own = columns(y_far, 0, 1, 0) + swap(y_far, next_core) + both_in
    y_in = swap(y_own, next_y)
    far = columns(y_own, 0, 0, 1)
    same = columns(far, 0, 0, 0) + swap(far, next_core) + x_in + y_in
    parts = lax.all_to_all(same.reshape(half * half, own, examples), "blk", 0, 0, axis_index_groups=alike, tiled=True)
    own_rows, partial = finish(parts, pair_index.T, 1.0 / math.sqrt(params * devices), 1.0 / math.sqrt(col_total))
    partial = partial + swap(partial, next_core)
    spread = jnp.broadcast_to(partial[None], (side * side,) + partial.shape)
    shares = lax.all_to_all(spread, "blk", 0, 0, axis_index_groups=chips, tiled=True)
    scores = jnp.sum(shares, axis=(0, 1))
    return (own_rows, scores)


def solution(mesh):
    placed = (P("grp", "blk"), P("blk", None), P("grp", None))
    return jax.shard_map(
        per_device,
        mesh=mesh,
        in_specs=placed,
        out_specs=(P("blk", "grp"), P("grp")),
        check_vma=False,
    )
```

time: 110 us -> 111 us (level)
  Pallas kernels: 47.1 us -> 40.4 us
  waiting for transfers between devices: 1.69 us -> 6.42 us
  starting transfers between devices: 24.9 us -> 27.4 us
    pallas_call x7 -> x10, Pallas kernels: 47.1 us -> 40.4 us  [the longest x8 39.6 us: project(): pl.pallas_call(functools.partial(project_kernel, own, half, params // TIL...]
    ppermute x6 -> x8, waiting for transfers between devices: 1.69 us -> 6.42 us  [swap(): return lax.ppermute(array, 'blk', [(d, d ^ flip) for d in range(devices)])]
    ppermute x6 -> x8, starting transfers between devices: 24.9 us -> 27.4 us  [swap(): return lax.ppermute(array, 'blk', [(d, d ^ flip) for d in range(devices)])]
    unnamed x7 -> x5, local copies, waits for them, and re-layouts: 2.36 us -> 1.51 us
  transfers between devices with their start and end apart: 6 -> 8, of which waited for: 3 -> 3; matrix products, arithmetic and copies ran while one was open for 0% -> 0% of each run, Pallas kernels for 32% -> 27%
where the time goes in v3:
time: 111 us; the launch traced here: 110 us
  Pallas kernels  40.4 us (36%)
  blocking collectives  33.2 us (30%)
  starting transfers between devices  27.4 us (25%)
  waiting for transfers between devices  6.42 us (6%)
  local copies, waits for them, and re-layouts  1.53 us (1%)
    pallas_call x8, Pallas kernels, project(): pl.pallas_call(functools.partial(project_kernel, own, half, params // TIL...  39.6 us
    ppermute x8, starting transfers between devices, swap(): return lax.ppermute(array, 'blk', [(d, d ^ flip) for d in range(devices)])  27.4 us
    all_to_all x1, blocking collectives, per_device(): lax.all_to_all(spread, 'blk', 0, 0, axis_index_groups=chips, tiled=True)  17.3 us
    all_to_all x1, blocking collectives, per_device(): lax.all_to_all(same.reshape(half * half, own, examples), 'blk', 0, 0, axi...  15.9 us
    ppermute x8, waiting for transfers between devices, swap(): return lax.ppermute(array, 'blk', [(d, d ^ flip) for d in range(devices)])  6.42 us
  transfers between devices with their start and end apart: 8, of which 3 were waited for; matrix products, arithmetic and copies ran while one was open for 0% of the time, Pallas kernels for 27%

profile of v3, /device:TPU:513, one launch (start us, length us, event | category | flops | bytes accessed | tf_op | source)
XLA Modules:
  0.0 110.4 jit_solution(1682355078248798220)
XLA Ops:
  0.6 0.0 copy-start.1
  0.6 0.9 copy.7.seeds_ref
  1.5 0.1 prepare.1.after_ref.seeds_ref
  1.6 0.6 copy-done.1
  2.2 5.0 %project.8.after_ref = f32[512,128]{1,0:T(8,128)S(1)} custom-call(s32[136,256]{1,0:T(8,128)S(1)} %prepare.1.after_ref.seeds_ref, s32[136,256]{1,0:T(8,128)S(1)} %prepare.1.after_ref.seeds_ref, bf16[128,8192]{1,0:T(8,128)(2,1)S(1)} %copy-done.1), custom_call_target="tpu_custom_call" | custom-call | flops 4294967296 | bytes 2097152 | tf_op jit(solution)/shard_map/project/pallas_call | solution.py:125
  7.2 20.5 %collective-permute-start = (f32[512,128]{1,0:T(8,128)S(1)}, f32[512,128]{1,0:T(8,128)S(1)}, u32[]{:S(2)}, u32[]{:S(2)}) collective-permute-start(f32[512,128]{1,0:T(8,128)S(1)} %project.8.after_ref), channel_id=1, source_target_pairs={{0,1},{1,0},{2,3},{3,2},{4,5},{5,4},{6,7},{7,6},{8,9},{9,8},{10,11... | collective-permute-start | bytes 786440 | tf_op jit(solution)/shard_map/ppermute | solution.py:184
  27.7 5.0 %project.9.after_ref = f32[512,128]{1,0:T(8,128)S(1)} custom-call(f32[512,128]{1,0:T(8,128)S(1)} %project.8.after_ref, s32[136,256]{1,0:T(8,128)S(1)} %prepare.1.after_ref.seeds_ref, bf16[128,8192]{1,0:T(8,128)(2,1)S(1)} %copy-done.1), custom_call_target="tpu_custom_call" | custom-call | flops 4294967296 | bytes 2097152 | tf_op jit(solution)/shard_map/project/pallas_call | solution.py:125
  32.7 0.2 collective-permute-start.1
  32.9 5.0 %project.10 = f32[512,128]{1,0:T(8,128)S(1)} custom-call(f32[512,128]{1,0:T(8,128)S(1)} %project.9.after_ref, s32[136,256]{1,0:T(8,128)S(1)} %prepare.1.after_ref.seeds_ref, bf16[128,8192]{1,0:T(8,128)(2,1)S(1)} %copy-done.1), custom_call_target="tpu_custom_call" | custom-call | flops 4294967296 | bytes 2097152 | tf_op jit(solution)/shard_map/project/pallas_call | solution.py:125
  37.8 0.0 collective-permute-done
  37.9 5.0 %project.11 = f32[512,128]{1,0:T(8,128)S(1)} custom-call(f32[512,128]{1,0:T(8,128)S(1)} %add.24.after_ref, s32[136,256]{1,0:T(8,128)S(1)} %prepare.1.after_ref.seeds_ref, bf16[128,8192]{1,0:T(8,128)(2,1)S(1)} %copy-done.1), custom_call_target="tpu_custom_call" | custom-call | flops 4294967296 | bytes 2097152 | tf_op jit(solution)/shard_map/project/pallas_call | solution.py:125
  42.8 0.0 collective-permute-done.1
  42.9 5.0 %project.12.after_ref = f32[512,128]{1,0:T(8,128)S(1)} custom-call(f32[512,128]{1,0:T(8,128)S(1)} %add.25.after_ref, s32[136,256]{1,0:T(8,128)S(1)} %prepare.1.after_ref.seeds_ref, bf16[128,8192]{1,0:T(8,128)(2,1)S(1)} %copy-done.1), custom_call_target="tpu_custom_call" | custom-call | flops 4294967296 | bytes 2097152 | tf_op jit(solution)/shard_map/project/pallas_call | solution.py:125
  47.8 0.1 collective-permute-start.5
  48.0 1.4 %collective-permute-start.3 = (f32[512,128]{1,0:T(8,128)S(1)}, f32[512,128]{1,0:T(8,128)S(1)}, u32[]{:S(2)}, u32[]{:S(2)}) collective-permute-start(f32[512,128]{1,0:T(8,128)S(1)} %add.24.after_ref), channel_id=1, source_target_pairs={{0,2},{1,3},{2,0},{3,1},{4,6},{5,7},{6,4},{7,5},{8,10},{9,11},{10,... | collective-permute-start | bytes 786440 | tf_op jit(solution)/shard_map/ppermute | solution.py:184
  49.4 1.0 collective-permute-start.2
  50.5 4.9 %project.13 = f32[512,128]{1,0:T(8,128)S(1)} custom-call(f32[512,128]{1,0:T(8,128)S(1)} %project.12.after_ref, s32[136,256]{1,0:T(8,128)S(1)} %prepare.1.after_ref.seeds_ref, bf16[128,8192]{1,0:T(8,128)(2,1)S(1)} %copy-done.1), custom_call_target="tpu_custom_call" | custom-call | flops 4294967296 | bytes 2097152 | tf_op jit(solution)/shard_map/project/pallas_call | solution.py:125
  55.4 0.0 collective-permute-done.2
  55.4 5.5 %collective-permute-done.3 = f32[512,128]{1,0:T(8,128)S(1)} collective-permute-done((f32[512,128]{1,0:T(8,128)S(1)}, f32[512,128]{1,0:T(8,128)S(1)}, u32[]{:S(2)}, u32[]{:S(2)}) %collective-permute-start.3) | collective-permute-done | bytes 262176 | tf_op jit(solution)/shard_map/ppermute | solution.py:184
  61.0 5.0 %project.14.after_ref = f32[512,128]{1,0:T(8,128)S(1)} custom-call(f32[512,128]{1,0:T(8,128)S(1)} %add_add_fusion.1.after_ref, s32[136,256]{1,0:T(8,128)S(1)} %prepare.1.after_ref.seeds_ref, bf16[128,8192]{1,0:T(8,128)(2,1)S(1)} %copy-done.1), custom_call_target="tpu_custom_call" | custom-call | flops 4294967296 | bytes 2097152 | tf_op jit(solution)/shard_map/project/pallas_call | solution.py:125
  66.0 0.0 copy-start
  66.0 0.1 collective-permute-start.6
  66.2 1.5 %collective-permute-start.4 = (f32[512,128]{1,0:T(8,128)S(1)}, f32[512,128]{1,0:T(8,128)S(1)}, u32[]{:S(2)}, u32[]{:S(2)}) collective-permute-start(f32[512,128]{1,0:T(8,128)S(1)} %project.14.after_ref), channel_id=1, source_target_pairs={{0,1},{1,0},{2,3},{3,2},{4,5},{5,4},{6,7},{7,6},{8,9},{9,8},{10,11... | collective-permute-start | bytes 786440 | tf_op jit(solution)/shard_map/ppermute | solution.py:184
  67.6 4.9 %project.15 = f32[512,128]{1,0:T(8,128)S(1)} custom-call(f32[512,128]{1,0:T(8,128)S(1)} %project.14.after_ref, s32[136,256]{1,0:T(8,128)S(1)} %prepare.1.after_ref.seeds_ref, bf16[128,8192]{1,0:T(8,128)(2,1)S(1)} %copy-done.1), custom_call_target="tpu_custom_call" | custom-call | flops 4294967296 | bytes 2097152 | tf_op jit(solution)/shard_map/project/pallas_call | solution.py:125
  72.6 0.0 collective-permute-done.5
  72.6 0.0 collective-permute-done.4
  72.6 0.1 collective-permute-done.6
  72.7 0.1 add_add_fusion
  72.7 15.9 %all_to_all.10.parts_ref = f32[16,32,128]{2,1,0:T(8,128)S(1)} all-to-all(f32[16,32,128]{2,1,0:T(8,128)S(1)} %bitcast.7), channel_id=1, replica_groups={{0,4,8,12,32,36,40,44,64,68,72,76,96,100,104,108},{1,5,9,13,33,37,41,45..., dimensions={0} | all-to-all | bytes 524288 | tf_op jit(solution)/shard_map/all_to_all | solution.py:211
  88.6 0.0 copy-done
  88.6 0.7 finish.1
  89.3 2.4 %collective-permute-start.7 = (f32[1,64]{1,0:T(1,128)S(1)}, f32[1,64]{1,0:T(1,128)S(1)}, u32[]{:S(2)}, u32[]{:S(2)}) collective-permute-start(f32[1,64]{1,0:T(1,128)S(1)} %get-tuple-element.5), channel_id=1, source_target_pairs={{0,1},{1,0},{2,3},{3,2},{4,5},{5,4},{6,7},{7,6},{8,9},{9,8},{10,11... | collective-permute-start | bytes 776 | tf_op jit(solution)/shard_map/ppermute | solution.py:184
  91.7 0.8 collective-permute-done.7
  92.5 17.3 %all_to_all.11 = f32[64,1,64]{2,1,0:T(1,128)S(1)} all-to-all(f32[64,1,64]{2,1,0:T(1,128)S(1)} %broadcast_in_dim.9), channel_id=1, replica_groups={{0,2,4,6,8,10,12,14,16,18,20,22,24,26,28,30,32,34,36,38,40,42,44,46,48,..., dimensions={0} | all-to-all | bytes 32768 | tf_op jit(solution)/shard_map/all_to_all | solution.py:215
  109.8 0.5 reduce_sum.9
  (5 shorter events, 0.1 us)
Async XLA Ops:
  0.6 1.6 %copy-start.1 = (bf16[128,8192]{1,0:T(8,128)(2,1)S(1)}, bf16[128,8192]{1,0:T(8,128)(2,1)}, u32[]{:S(2)}) copy-start(bf16[128,8192]{1,0:T(8,128)(2,1)} %grads_ref.15) | copy-start | bytes 6291460
  7.2 30.6 %collective-permute-start = (f32[512,128]{1,0:T(8,128)S(1)}, f32[512,128]{1,0:T(8,128)S(1)}, u32[]{:S(2)}, u32[]{:S(2)}) collective-permute-start(f32[512,128]{1,0:T(8,128)S(1)} %project.8.after_ref), channel_id=1, source_target_pairs={{0,1},{1,0},{2,3},{3,2},{4,5},{5,4},{6,7},{7,6},{8,9},{9,8},{10,11... | collective-permute-start | bytes 786440 | tf_op jit(solution)/shard_map/ppermute | solution.py:184
  32.7 10.1 %collective-permute-start.1 = (f32[512,128]{1,0:T(8,128)S(1)}, f32[512,128]{1,0:T(8,128)S(1)}, u32[]{:S(2)}, u32[]{:S(2)}) collective-permute-start(f32[512,128]{1,0:T(8,128)S(1)} %project.9.after_ref), channel_id=1, source_target_pairs={{0,1},{1,0},{2,3},{3,2},{4,5},{5,4},{6,7},{7,6},{8,9},{9,8},{10,11... | collective-permute-start | bytes 786440 | tf_op jit(solution)/shard_map/ppermute | solution.py:184
  47.8 24.7 %collective-permute-start.5 = (f32[512,128]{1,0:T(8,128)S(1)}, f32[512,128]{1,0:T(8,128)S(1)}, u32[]{:S(2)}, u32[]{:S(2)}) collective-permute-start(f32[512,128]{1,0:T(8,128)S(1)} %add.25.after_ref), channel_id=1, source_target_pairs={{0,2},{1,3},{2,0},{3,1},{4,6},{5,7},{6,4},{7,5},{8,10},{9,11},{10,... | collective-permute-start | bytes 786440 | tf_op jit(solution)/shard_map/ppermute | solution.py:184
  48.0 13.0 %collective-permute-start.3 = (f32[512,128]{1,0:T(8,128)S(1)}, f32[512,128]{1,0:T(8,128)S(1)}, u32[]{:S(2)}, u32[]{:S(2)}) collective-permute-start(f32[512,128]{1,0:T(8,128)S(1)} %add.24.after_ref), channel_id=1, source_target_pairs={{0,2},{1,3},{2,0},{3,1},{4,6},{5,7},{6,4},{7,5},{8,10},{9,11},{10,... | collective-permute-start | bytes 786440 | tf_op jit(solution)/shard_map/ppermute | solution.py:184
  49.4 6.0 %collective-permute-start.2 = (f32[512,128]{1,0:T(8,128)S(1)}, f32[512,128]{1,0:T(8,128)S(1)}, u32[]{:S(2)}, u32[]{:S(2)}) collective-permute-start(f32[512,128]{1,0:T(8,128)S(1)} %project.12.after_ref), channel_id=1, source_target_pairs={{0,1},{1,0},{2,3},{3,2},{4,5},{5,4},{6,7},{7,6},{8,9},{9,8},{10,11... | collective-permute-start | bytes 786440 | tf_op jit(solution)/shard_map/ppermute | solution.py:184
  66.0 22.6 %copy-start = (s32[64,2]{0,1:T(2,128)S(1)}, s32[64,2]{0,1:T(2,128)}, u32[]{:S(2)}) copy-start(s32[64,2]{0,1:T(2,128)} %param.5) | copy-start | bytes 1540
  66.0 6.6 %collective-permute-start.6 = (f32[512,128]{1,0:T(8,128)S(1)}, f32[512,128]{1,0:T(8,128)S(1)}, u32[]{:S(2)}, u32[]{:S(2)}) collective-permute-start(f32[512,128]{1,0:T(8,128)S(1)} %add_add_fusion.1.after_ref), channel_id=1, source_target_pairs={{0,16},{1,17},{2,18},{3,19},{4,20},{5,21},{6,22},{7,23},{8,24},{9,... | collective-permute-start | bytes 786440 | tf_op jit(solution)/shard_map/ppermute | solution.py:184
  66.2 6.4 %collective-permute-start.4 = (f32[512,128]{1,0:T(8,128)S(1)}, f32[512,128]{1,0:T(8,128)S(1)}, u32[]{:S(2)}, u32[]{:S(2)}) collective-permute-start(f32[512,128]{1,0:T(8,128)S(1)} %project.14.after_ref), channel_id=1, source_target_pairs={{0,1},{1,0},{2,3},{3,2},{4,5},{5,4},{6,7},{7,6},{8,9},{9,8},{10,11... | collective-permute-start | bytes 786440 | tf_op jit(solution)/shard_map/ppermute | solution.py:184
  89.3 3.3 %collective-permute-start.7 = (f32[1,64]{1,0:T(1,128)S(1)}, f32[1,64]{1,0:T(1,128)S(1)}, u32[]{:S(2)}, u32[]{:S(2)}) collective-permute-start(f32[1,64]{1,0:T(1,128)S(1)} %get-tuple-element.5), channel_id=1, source_target_pairs={{0,1},{1,0},{2,3},{3,2},{4,5},{5,4},{6,7},{7,6},{8,9},{9,8},{10,11... | collective-permute-start | bytes 776 | tf_op jit(solution)/shard_map/ppermute | solution.py:184

commit v4 on v3

--- a/solution.py
+++ b/solution.py
@@ -19,20 +19,26 @@
 mixer_two = -1028477387
 
 
-def signs(table, seed):
+def minus_two_bits(table, seed):
     mixed = (table ^ seed) * jnp.int32(mixer_one)
     mixed = mixed ^ lax.shift_right_logical(mixed, jnp.int32(13))
     mixed = mixed * jnp.int32(mixer_two)
     mixed = mixed ^ lax.shift_right_logical(mixed, jnp.int32(16))
-    return jnp.where(mixed.astype(jnp.int16) < 0, jnp.bfloat16(-1), jnp.bfloat16(1))
-
-
-def prepare_kernel(half, side, me_ref, seeds_ref, rows_ref):
+    return jnp.where(mixed.astype(jnp.int16) < 0, jnp.bfloat16(-2), jnp.bfloat16(0))
+
+
+def prepare_kernel(half, side, own, me_ref, seeds_ref, rows_ref, tables_ref):
     tiles = seeds_ref.shape[0]
     me = me_ref[0]
     own_y = (me // (CORES * side)) & 1
-    last = 2 * half * tiles
-    rows_ref[last:, :] = jnp.full((rows_ref.shape[0] - last, WIDTH), me & (2 * CORES - 1), jnp.int32)
+    shape = (half * own, TILE)
+    row = lax.broadcasted_iota(jnp.int32, shape, 0)
+    param = lax.broadcasted_iota(jnp.int32, shape, 1)
+    index = param * TILE + (row // own) * (2 * CORES * own) + row % own
+    for flip in range(2 * CORES):
+        place = (me & (2 * CORES - 1)) ^ flip
+        product = (index + place * own) * jnp.int32(golden_mult)
+        tables_ref[flip * half * own : (flip + 1) * half * own, :] = product ^ lax.shift_right_logical(product, jnp.int32(16))
     seeds = seeds_ref[...]
     seeds = seeds ^ lax.shift_right_logical(seeds, jnp.int32(16))
     for y in range(2 * half):
@@ -40,41 +46,37 @@
         rows_ref[pl.ds(row, tiles), :] = jnp.broadcast_to(seeds[:, y : y + 1], (tiles, WIDTH))
 
 
-def prepare(me, seeds, side):
+def prepare(me, seeds, side, own):
     half = side // 2
     vmem = pl.BlockSpec(memory_space=pltpu.VMEM)
     return pl.pallas_call(
-        functools.partial(prepare_kernel, half, side),
-        out_shape=jax.ShapeDtypeStruct((2 * seeds.shape[0] * half + 8, WIDTH), jnp.int32),
+        functools.partial(prepare_kernel, half, side, own),
+        out_shape=(
+            jax.ShapeDtypeStruct((2 * half * seeds.shape[0], WIDTH), jnp.int32),
+            jax.ShapeDtypeStruct((2 * CORES * half * own, TILE), jnp.int32),
+        ),
         in_specs=[pl.BlockSpec(memory_space=pltpu.SMEM), vmem],
-        out_specs=vmem,
+        out_specs=(vmem, vmem),
         compiler_params=pltpu.CompilerParams(vmem_limit_bytes=12 << 20),
         cost_estimate=pl.CostEstimate(flops=1 << 30, bytes_accessed=1 << 16, transcendentals=0),
         name="prepare",
     )(me, seeds)
 
 
-def project_kernel(own, half, tiles, flips, after_ref, seeds_ref, grads_ref, out_ref, table):
+def project_kernel(own, half, tiles, flips, first, after_ref, seeds_ref, tables_ref, grads_ref, out_ref):
     del after_ref
     x_flip, y_flip, core_flip = flips
     examples = grads_ref.shape[0]
-    tile_rows = table.shape[0]
-    unit_rows = half * tile_rows
-    pieces = unit_rows // PIECE
+    tile_rows = half * own
+    table = tables_ref.at[(x_flip * CORES + core_flip) * tile_rows : (x_flip * CORES + core_flip + 1) * tile_rows, :]
+    pieces = half * tile_rows // PIECE
     parts = TILE // WIDTH
 
     def run(*sums):
-        acc = [sums[part * pieces : (part + 1) * pieces] for part in range(parts)]
-        for part in range(parts):
-            for one in acc[part]:
+        acc = [sums[part * (pieces + 1) : (part + 1) * (pieces + 1)] for part in range(parts)]
+        if first:
+            for one in sums:
                 pltpu.matmul_pop(one)
-        place = seeds_ref[2 * tiles * half : 2 * tiles * half + 1, :] ^ (x_flip * CORES + core_flip)
-        row = lax.broadcasted_iota(jnp.int32, (tile_rows, WIDTH), 0)
-        column = (row // own) * (2 * CORES * own) + row % own + place * own
-        for start in range(0, TILE, WIDTH):
-            param = lax.broadcasted_iota(jnp.int32, (tile_rows, WIDTH), 1) + start
-            product = (param * TILE + column) * jnp.int32(golden_mult)
-            table[:, start : start + WIDTH] = product ^ lax.shift_right_logical(product, jnp.int32(16))
 
         def push(tile):
             for part in range(parts):
@@ -83,6 +85,10 @@
                 pltpu.matmul_push_rhs(block, staging_register=0, mxu_index=part, transpose=True)
 
         def tile_step(first_seed, tile, following):
+            for part in range(parts):
+                pltpu.matmul_acc_lhs(acc[part][pieces], jnp.ones((PIECE, WIDTH), jnp.bfloat16), load_staged_rhs=0)
+            if following is not None:
+                push(following)
             for i in range(half):
                 seed = seeds_ref[pl.ds(first_seed + i * tiles + tile, 1), :]
                 for start in range(0, tile_rows, PIECE):
@@ -90,11 +96,8 @@
                     for part in range(parts):
                         pltpu.matmul_acc_lhs(
                             acc[part][piece],
-                            signs(table[start : start + PIECE, part * WIDTH : (part + 1) * WIDTH], seed),
-                            load_staged_rhs=0 if piece == 0 else None,
+                            minus_two_bits(table[start : start + PIECE, part * WIDTH : (part + 1) * WIDTH], seed),
                         )
-                    if piece == 0 and following is not None:
-                        push(following)
 
         first_seed = y_flip * half * tiles
         push(0)
@@ -107,33 +110,31 @@
         lax.fori_loop(0, tiles // 2 - 1, pair_step, 0)
         tile_step(first_seed, tiles - 2, tiles - 1)
         tile_step(first_seed, tiles - 1, None)
+        whole = sum(pltpu.matmul_pop(acc[part][pieces])[:, :examples] for part in range(parts))
         for piece in range(pieces):
-            total = pltpu.matmul_pop(acc[0][piece])[:, :examples]
-            for part in range(1, parts):
-                total = total + pltpu.matmul_pop(acc[part][piece])[:, :examples]
-            out_ref[piece * PIECE : (piece + 1) * PIECE, :] = total
-
-    pl.run_scoped(run, *[pltpu.ACC(part)((PIECE, WIDTH), jnp.float32) for part in range(parts) for _ in range(pieces)])
-
-
-def project(after, seeds, grads, own, side, flips):
+            total = sum(pltpu.matmul_pop(acc[part][piece])[:, :examples] for part in range(parts))
+            out_ref[piece * PIECE : (piece + 1) * PIECE, :] = whole + total
+
+    pl.run_scoped(run, *[pltpu.ACC(part)((PIECE, WIDTH), jnp.float32) for part in range(parts) for _ in range(pieces + 1)])
+
+
+def project(after, seeds, tables, grads, own, side, flips):
     examples, params = grads.shape
     half = side // 2
     tile_rows = half * own
     rows = half * tile_rows
     vmem = pl.BlockSpec(memory_space=pltpu.VMEM)
     return pl.pallas_call(
-        functools.partial(project_kernel, own, half, params // TILE, flips),
+        functools.partial(project_kernel, own, half, params // TILE, flips, after is seeds),
         out_shape=jax.ShapeDtypeStruct((rows, examples), jnp.float32),
-        in_specs=[vmem, vmem, vmem],
+        in_specs=[vmem] * 4,
         out_specs=vmem,
-        scratch_shapes=[pltpu.VMEM((tile_rows, TILE), jnp.int32)],
         compiler_params=pltpu.CompilerParams(vmem_limit_bytes=12 << 20),
         cost_estimate=pl.CostEstimate(
             flops=8 * rows * examples * params, bytes_accessed=2 * examples * params, transcendentals=0
         ),
         name="project",
-    )(after, seeds, grads)
+    )(after, seeds, tables, grads)
 
 
 def finish_kernel(scaling, score_scaling, parts_ref, pairs_ref, own_ref, score_ref):
@@ -183,7 +184,7 @@
     def swap(array, flip):
         return lax.ppermute(array, "blk", [(d, d ^ flip) for d in range(devices)])
 
-    seeds = prepare(me, tile_seeds, side)
+    seeds, tables = prepare(me, tile_seeds, side, own)
 
     alike = [
         [place(2 * i + py, 2 * j + px, c) for i in range(half) for j in range(half)]
@@ -195,7 +196,7 @@
     next_core, next_x, next_y = 1, CORES, CORES * side
 
     def columns(after, x_flip, y_flip, core_flip):
-        return project(after, seeds, example_grads, own, side, (x_flip, y_flip, core_flip))
+        return project(after, seeds, tables, example_grads, own, side, (x_flip, y_flip, core_flip))
 
     both_far = columns(seeds, 1, 1, 1)
     x_far = columns(both_far, 1, 0, 1)

time: 111 us -> 108 us (0.973)
  Pallas kernels: 40.4 us -> 38.2 us
    pallas_call x8, Pallas kernels: 39.6 us -> 37.2 us  [project(): pl.pallas_call(functools.partial(project_kernel, own, half, params // TIL...]
  transfers between devices with their start and end apart: 8 -> 8, of which waited for: 3 -> 3; matrix products, arithmetic and copies ran while one was open for 0% -> 0% of each run, Pallas kernels for 27% -> 26%
where the time goes in v4:
time: 108 us
  Pallas kernels  38.2 us (35%)
  blocking collectives  32.6 us (30%)
  starting transfers between devices  27.3 us (25%)
  waiting for transfers between devices  7.01 us (6%)
  local copies, waits for them, and re-layouts  1.33 us (1%)
    pallas_call x8, Pallas kernels, project(): pl.pallas_call(functools.partial(project_kernel, own, half, params // TIL...  37.2 us
    ppermute x8, starting transfers between devices, swap(): return lax.ppermute(array, 'blk', [(d, d ^ flip) for d in range(devices)])  27.3 us
    all_to_all x1, blocking collectives, per_device(): lax.all_to_all(spread, 'blk', 0, 0, axis_index_groups=chips, tiled=True)  16.7 us
    all_to_all x1, blocking collectives, per_device(): lax.all_to_all(same.reshape(half * half, own, examples), 'blk', 0, 0, axi...  15.9 us
    ppermute x8, waiting for transfers between devices, swap(): return lax.ppermute(array, 'blk', [(d, d ^ flip) for d in range(devices)])  7.01 us
  transfers between devices with their start and end apart: 8, of which 3 were waited for; matrix products, arithmetic and copies ran while one was open for 0% of the time, Pallas kernels for 26%

profile of v4, /device:TPU:513, one launch (start us, length us, event | category | flops | bytes accessed | tf_op | source)
XLA Modules:
  0.0 107.9 jit_solution(12298858702199027517)
XLA Ops:
  0.6 0.0 copy-start.1
  0.6 0.9 copy.7.seeds_ref
  1.5 0.3 prepare.1
  1.8 0.4 copy-done.1
  2.2 4.7 %project.8.after_ref = f32[512,128]{1,0:T(8,128)S(1)} custom-call(s32[128,256]{1,0:T(8,128)S(1)} %get-tuple-element.6.after_ref.seeds_ref, s32[128,256]{1,0:T(8,128)S(1)} %get-tuple-element.6.after_ref.seeds_ref, s32[512,512]{1,0:T(8,128)S(1)} %get-tuple-element.7.tables_ref, bf16[128,8192]{1,0:T(8,128)(2,1)S(1)} %copy-done.1), custom_call_target="tpu_custom_call" | custom-call | flops 4294967296 | bytes 2097152 | tf_op jit(solution)/shard_map/project/pallas_call | solution.py:127
  6.9 20.5 %collective-permute-start = (f32[512,128]{1,0:T(8,128)S(1)}, f32[512,128]{1,0:T(8,128)S(1)}, u32[]{:S(2)}, u32[]{:S(2)}) collective-permute-start(f32[512,128]{1,0:T(8,128)S(1)} %project.8.after_ref), channel_id=1, source_target_pairs={{0,1},{1,0},{2,3},{3,2},{4,5},{5,4},{6,7},{7,6},{8,9},{9,8},{10,11... | collective-permute-start | bytes 786440 | tf_op jit(solution)/shard_map/ppermute | solution.py:185
  27.4 4.7 %project.9.after_ref = f32[512,128]{1,0:T(8,128)S(1)} custom-call(f32[512,128]{1,0:T(8,128)S(1)} %project.8.after_ref, s32[128,256]{1,0:T(8,128)S(1)} %get-tuple-element.6.after_ref.seeds_ref, s32[512,512]{1,0:T(8,128)S(1)} %get-tuple-element.7.tables_ref, bf16[128,8192]{1,0:T(8,128)(2,1)S(1)} %copy-done.1), custom_call_target="tpu_custom_call" | custom-call | flops 4294967296 | bytes 2097152 | tf_op jit(solution)/shard_map/project/pallas_call | solution.py:127
  32.1 0.2 collective-permute-start.1
  32.3 4.6 %project.10 = f32[512,128]{1,0:T(8,128)S(1)} custom-call(f32[512,128]{1,0:T(8,128)S(1)} %project.9.after_ref, s32[128,256]{1,0:T(8,128)S(1)} %get-tuple-element.6.after_ref.seeds_ref, s32[512,512]{1,0:T(8,128)S(1)} %get-tuple-element.7.tables_ref, bf16[128,8192]{1,0:T(8,128)(2,1)S(1)} %copy-done.1), custom_call_target="tpu_custom_call" | custom-call | flops 4294967296 | bytes 2097152 | tf_op jit(solution)/shard_map/project/pallas_call | solution.py:127
  36.9 0.0 collective-permute-done
  37.0 4.7 %project.11 = f32[512,128]{1,0:T(8,128)S(1)} custom-call(f32[512,128]{1,0:T(8,128)S(1)} %add.24.after_ref, s32[128,256]{1,0:T(8,128)S(1)} %get-tuple-element.6.after_ref.seeds_ref, s32[512,512]{1,0:T(8,128)S(1)} %get-tuple-element.7.tables_ref, bf16[128,8192]{1,0:T(8,128)(2,1)S(1)} %copy-done.1), custom_call_target="tpu_custom_call" | custom-call | flops 4294967296 | bytes 2097152 | tf_op jit(solution)/shard_map/project/pallas_call | solution.py:127
  41.6 0.0 collective-permute-done.1
  41.7 4.6 %project.12.after_ref = f32[512,128]{1,0:T(8,128)S(1)} custom-call(f32[512,128]{1,0:T(8,128)S(1)} %add.25.after_ref, s32[128,256]{1,0:T(8,128)S(1)} %get-tuple-element.6.after_ref.seeds_ref, s32[512,512]{1,0:T(8,128)S(1)} %get-tuple-element.7.tables_ref, bf16[128,8192]{1,0:T(8,128)(2,1)S(1)} %copy-done.1), custom_call_target="tpu_custom_call" | custom-call | flops 4294967296 | bytes 2097152 | tf_op jit(solution)/shard_map/project/pallas_call | solution.py:127
  46.3 0.1 collective-permute-start.5
  46.5 1.4 %collective-permute-start.3 = (f32[512,128]{1,0:T(8,128)S(1)}, f32[512,128]{1,0:T(8,128)S(1)}, u32[]{:S(2)}, u32[]{:S(2)}) collective-permute-start(f32[512,128]{1,0:T(8,128)S(1)} %add.24.after_ref), channel_id=1, source_target_pairs={{0,2},{1,3},{2,0},{3,1},{4,6},{5,7},{6,4},{7,5},{8,10},{9,11},{10,... | collective-permute-start | bytes 786440 | tf_op jit(solution)/shard_map/ppermute | solution.py:185
  47.9 1.0 collective-permute-start.2
  49.0 4.6 %project.13 = f32[512,128]{1,0:T(8,128)S(1)} custom-call(f32[512,128]{1,0:T(8,128)S(1)} %project.12.after_ref, s32[128,256]{1,0:T(8,128)S(1)} %get-tuple-element.6.after_ref.seeds_ref, s32[512,512]{1,0:T(8,128)S(1)} %get-tuple-element.7.tables_ref, bf16[128,8192]{1,0:T(8,128)(2,1)S(1)} %copy-done.1), custom_call_target="tpu_custom_call" | custom-call | flops 4294967296 | bytes 2097152 | tf_op jit(solution)/shard_map/project/pallas_call | solution.py:127
  53.6 0.0 collective-permute-done.2
  53.6 5.8 %collective-permute-done.3 = f32[512,128]{1,0:T(8,128)S(1)} collective-permute-done((f32[512,128]{1,0:T(8,128)S(1)}, f32[512,128]{1,0:T(8,128)S(1)}, u32[]{:S(2)}, u32[]{:S(2)}) %collective-permute-start.3) | collective-permute-done | bytes 262176 | tf_op jit(solution)/shard_map/ppermute | solution.py:185
  59.5 4.7 %project.14.after_ref = f32[512,128]{1,0:T(8,128)S(1)} custom-call(f32[512,128]{1,0:T(8,128)S(1)} %add_add_fusion.1.after_ref, s32[128,256]{1,0:T(8,128)S(1)} %get-tuple-element.6.after_ref.seeds_ref, s32[512,512]{1,0:T(8,128)S(1)} %get-tuple-element.7.tables_ref, bf16[128,8192]{1,0:T(8,128)(2,1)S(1)} %copy-done.1), custom_call_target="tpu_custom_call" | custom-call | flops 4294967296 | bytes 2097152 | tf_op jit(solution)/shard_map/project/pallas_call | solution.py:127
  64.2 0.0 copy-start
  64.2 0.1 collective-permute-start.6
  64.3 1.5 %collective-permute-start.4 = (f32[512,128]{1,0:T(8,128)S(1)}, f32[512,128]{1,0:T(8,128)S(1)}, u32[]{:S(2)}, u32[]{:S(2)}) collective-permute-start(f32[512,128]{1,0:T(8,128)S(1)} %project.14.after_ref), channel_id=1, source_target_pairs={{0,1},{1,0},{2,3},{3,2},{4,5},{5,4},{6,7},{7,6},{8,9},{9,8},{10,11... | collective-permute-start | bytes 786440 | tf_op jit(solution)/shard_map/ppermute | solution.py:185
  65.8 4.7 %project.15 = f32[512,128]{1,0:T(8,128)S(1)} custom-call(f32[512,128]{1,0:T(8,128)S(1)} %project.14.after_ref, s32[128,256]{1,0:T(8,128)S(1)} %get-tuple-element.6.after_ref.seeds_ref, s32[512,512]{1,0:T(8,128)S(1)} %get-tuple-element.7.tables_ref, bf16[128,8192]{1,0:T(8,128)(2,1)S(1)} %copy-done.1), custom_call_target="tpu_custom_call" | custom-call | flops 4294967296 | bytes 2097152 | tf_op jit(solution)/shard_map/project/pallas_call | solution.py:127
  70.5 0.0 collective-permute-done.5
  70.5 0.0 collective-permute-done.4
  70.5 0.4 collective-permute-done.6
  70.9 15.9 %all_to_all.10.parts_ref = f32[16,32,128]{2,1,0:T(8,128)S(1)} all-to-all(f32[16,32,128]{2,1,0:T(8,128)S(1)} %bitcast.7), channel_id=1, replica_groups={{0,4,8,12,32,36,40,44,64,68,72,76,96,100,104,108},{1,5,9,13,33,37,41,45..., dimensions={0} | all-to-all | bytes 524288 | tf_op jit(solution)/shard_map/all_to_all | solution.py:212
  86.8 0.0 copy-done
  86.8 0.7 finish.1
  87.5 2.4 %collective-permute-start.7 = (f32[1,64]{1,0:T(1,128)S(1)}, f32[1,64]{1,0:T(1,128)S(1)}, u32[]{:S(2)}, u32[]{:S(2)}) collective-permute-start(f32[1,64]{1,0:T(1,128)S(1)} %get-tuple-element.9), channel_id=1, source_target_pairs={{0,1},{1,0},{2,3},{3,2},{4,5},{5,4},{6,7},{7,6},{8,9},{9,8},{10,11... | collective-permute-start | bytes 776 | tf_op jit(solution)/shard_map/ppermute | solution.py:185
  89.9 0.8 collective-permute-done.7
  90.7 16.7 %all_to_all.11 = f32[64,1,64]{2,1,0:T(1,128)S(1)} all-to-all(f32[64,1,64]{2,1,0:T(1,128)S(1)} %broadcast_in_dim.9), channel_id=1, replica_groups={{0,2,4,6,8,10,12,14,16,18,20,22,24,26,28,30,32,34,36,38,40,42,44,46,48,..., dimensions={0} | all-to-all | bytes 32768 | tf_op jit(solution)/shard_map/all_to_all | solution.py:216
  107.4 0.5 reduce_sum.9
  (6 shorter events, 0.2 us)
Async XLA Ops:
  0.6 1.6 %copy-start.1 = (bf16[128,8192]{1,0:T(8,128)(2,1)S(1)}, bf16[128,8192]{1,0:T(8,128)(2,1)}, u32[]{:S(2)}) copy-start(bf16[128,8192]{1,0:T(8,128)(2,1)} %grads_ref.15) | copy-start | bytes 6291460
  6.9 30.0 %collective-permute-start = (f32[512,128]{1,0:T(8,128)S(1)}, f32[512,128]{1,0:T(8,128)S(1)}, u32[]{:S(2)}, u32[]{:S(2)}) collective-permute-start(f32[512,128]{1,0:T(8,128)S(1)} %project.8.after_ref), channel_id=1, source_target_pairs={{0,1},{1,0},{2,3},{3,2},{4,5},{5,4},{6,7},{7,6},{8,9},{9,8},{10,11... | collective-permute-start | bytes 786440 | tf_op jit(solution)/shard_map/ppermute | solution.py:185
  32.1 9.5 %collective-permute-start.1 = (f32[512,128]{1,0:T(8,128)S(1)}, f32[512,128]{1,0:T(8,128)S(1)}, u32[]{:S(2)}, u32[]{:S(2)}) collective-permute-start(f32[512,128]{1,0:T(8,128)S(1)} %project.9.after_ref), channel_id=1, source_target_pairs={{0,1},{1,0},{2,3},{3,2},{4,5},{5,4},{6,7},{7,6},{8,9},{9,8},{10,11... | collective-permute-start | bytes 786440 | tf_op jit(solution)/shard_map/ppermute | solution.py:185
  46.3 24.1 %collective-permute-start.5 = (f32[512,128]{1,0:T(8,128)S(1)}, f32[512,128]{1,0:T(8,128)S(1)}, u32[]{:S(2)}, u32[]{:S(2)}) collective-permute-start(f32[512,128]{1,0:T(8,128)S(1)} %add.25.after_ref), channel_id=1, source_target_pairs={{0,2},{1,3},{2,0},{3,1},{4,6},{5,7},{6,4},{7,5},{8,10},{9,11},{10,... | collective-permute-start | bytes 786440 | tf_op jit(solution)/shard_map/ppermute | solution.py:185
  46.5 13.0 %collective-permute-start.3 = (f32[512,128]{1,0:T(8,128)S(1)}, f32[512,128]{1,0:T(8,128)S(1)}, u32[]{:S(2)}, u32[]{:S(2)}) collective-permute-start(f32[512,128]{1,0:T(8,128)S(1)} %add.24.after_ref), channel_id=1, source_target_pairs={{0,2},{1,3},{2,0},{3,1},{4,6},{5,7},{6,4},{7,5},{8,10},{9,11},{10,... | collective-permute-start | bytes 786440 | tf_op jit(solution)/shard_map/ppermute | solution.py:185
  47.9 5.7 %collective-permute-start.2 = (f32[512,128]{1,0:T(8,128)S(1)}, f32[512,128]{1,0:T(8,128)S(1)}, u32[]{:S(2)}, u32[]{:S(2)}) collective-permute-start(f32[512,128]{1,0:T(8,128)S(1)} %project.12.after_ref), channel_id=1, source_target_pairs={{0,1},{1,0},{2,3},{3,2},{4,5},{5,4},{6,7},{7,6},{8,9},{9,8},{10,11... | collective-permute-start | bytes 786440 | tf_op jit(solution)/shard_map/ppermute | solution.py:185
  64.2 22.6 %copy-start = (s32[64,2]{0,1:T(2,128)S(1)}, s32[64,2]{0,1:T(2,128)}, u32[]{:S(2)}) copy-start(s32[64,2]{0,1:T(2,128)} %param.5) | copy-start | bytes 1540
  64.2 6.6 %collective-permute-start.6 = (f32[512,128]{1,0:T(8,128)S(1)}, f32[512,128]{1,0:T(8,128)S(1)}, u32[]{:S(2)}, u32[]{:S(2)}) collective-permute-start(f32[512,128]{1,0:T(8,128)S(1)} %add_add_fusion.1.after_ref), channel_id=1, source_target_pairs={{0,16},{1,17},{2,18},{3,19},{4,20},{5,21},{6,22},{7,23},{8,24},{9,... | collective-permute-start | bytes 786440 | tf_op jit(solution)/shard_map/ppermute | solution.py:185
  64.3 6.1 %collective-permute-start.4 = (f32[512,128]{1,0:T(8,128)S(1)}, f32[512,128]{1,0:T(8,128)S(1)}, u32[]{:S(2)}, u32[]{:S(2)}) collective-permute-start(f32[512,128]{1,0:T(8,128)S(1)} %project.14.after_ref), channel_id=1, source_target_pairs={{0,1},{1,0},{2,3},{3,2},{4,5},{5,4},{6,7},{7,6},{8,9},{9,8},{10,11... | collective-permute-start | bytes 786440 | tf_op jit(solution)/shard_map/ppermute | solution.py:185
  87.5 3.2 %collective-permute-start.7 = (f32[1,64]{1,0:T(1,128)S(1)}, f32[1,64]{1,0:T(1,128)S(1)}, u32[]{:S(2)}, u32[]{:S(2)}) collective-permute-start(f32[1,64]{1,0:T(1,128)S(1)} %get-tuple-element.9), channel_id=1, source_target_pairs={{0,1},{1,0},{2,3},{3,2},{4,5},{5,4},{6,7},{7,6},{8,9},{9,8},{10,11... | collective-permute-start | bytes 776 | tf_op jit(solution)/shard_map/ppermute | solution.py:185
